TPU v7x, 768 devices: a whole 4x8x12 slice. The times are simulated.
768 devices in a mesh: gx: 48 (over x, z), gy: 2 (over core), gz: 8 (over y).
Axes of the slice: x: 4, y: 8, z: 12, core: 2. Of those that a mesh axis runs over, the one named last changes fastest.
Arguments:
- density: int32 [192, 32, 1024], P('gx', 'gy', 'gz'), may hold values from 0 to 15
- fixed_mask: int32 [192, 32, 1024], P('gx', 'gy', 'gz'), may hold values from 0 to 1, as said below
- load_mask: int32 [192, 32, 1024], P('gx', 'gy', 'gz'), may hold values 0 or 1
- forces: float32 [3, 192, 32, 1024], P(None, 'gx', 'gy', 'gz'), may hold values from -6 to 6
Outputs:
- displacement: float32 [3, 192, 32, 1024], P(None, 'gx', 'gy', 'gz')
- residual: float32 [3, 192, 32, 1024], P(None, 'gx', 'gy', 'gz')
Inputs may be any that keep to these rules, and one draw needn't show every extreme that they name: `fixed_mask`: supports stand only on voxels whose first index is 0 or 1.
All inputs are finite; a program needn't handle non-finite values. No bound on the sum of `load_mask` on one device may be relied on, other than what follows from the above.
Results may differ from a plain program's by a relative error of at most 0.0003.
Values sent between devices are 32-bit elements; how exact they have to be, the bound alone decides.
A program may use at most 32 MiB of HBM per device.

v0:
```python
import jax
import jax.numpy as jnp
from jax import lax
from jax.sharding import Mesh
from jax.sharding import PartitionSpec as P

ITERS = 2
GX = ("gx_0", "gx_1")
GX_GY_GZ = ("gx_0", "gx_1", "gy", "gz")


LAME = 0.5
PENALTY = 4.0
OMEGA = 0.5
unit_steps = ((1, 0, 0), (0, 1, 0), (0, 0, 1))


def extended(x, sides, width):
    edges = {}
    for axis, dim in sides:
        count, length = (lax.axis_size(axis), x.shape[dim])
        up = [(i, (i + 1) % count) for i in range(count - 1)]
        last = lax.slice_in_dim(x, length - width, length, axis=dim)
        first = lax.slice_in_dim(x, 0, width, axis=dim)
        edges[dim] = (
            lax.ppermute(last, axis, up),
            lax.ppermute(first, axis, [(b, a) for a, b in up]),
        )
    done = []
    for _, dim in sides:
        low, high = edges[dim]
        around = [(width, width) if d in done else (0, 0) for d in range(x.ndim)]
        x = jnp.concatenate([jnp.pad(low, around), x, jnp.pad(high, around)], axis=dim)
        done.append(dim)
    return x


def with_halo(block, sides, width):
    for axis, dim in sides:
        count = lax.axis_size(axis)
        forward = [(i, i + 1) for i in range(count - 1)]
        backward = [(target, source) for source, target in forward]
        low = lax.ppermute(
            lax.slice_in_dim(block, block.shape[dim] - width, None, axis=dim), axis, forward
        )
        high = lax.ppermute(lax.slice_in_dim(block, 0, width, axis=dim), axis, backward)
        block = jnp.concatenate([low, block, high], axis=dim)
    return block


def copy_for_each(x, axis):
    copies = jnp.broadcast_to(x, (lax.axis_size(axis), *x.shape))
    return lax.all_to_all(copies, axis, split_axis=0, concat_axis=0, tiled=True)


def over_copies(x, axis):
    return copy_for_each(x, axis).sum(axis=0)


def joined_along(tiles, dim):
    tiles = jnp.moveaxis(tiles, 0, dim)
    dims = tiles.shape
    return tiles.reshape(*dims[:dim], dims[dim] * dims[dim + 1], *dims[dim + 2 :])


def collect(x, axis, dim):
    return joined_along(copy_for_each(x, axis), dim)


def by_axis(x, axes):
    for axis in axes:
        x = lax.psum(x, axis)
    return x


def modulus(density):
    level = density.astype(jnp.float32) / 15.0
    return 0.05 + 0.95 * level * level * level


def shifted(padded, step_x, step_y, step_z):
    size_x = padded.shape[-3] - 2
    size_y = padded.shape[-2] - 2
    size_z = padded.shape[-1] - 2
    return padded[
        ...,
        1 + step_x : 1 + step_x + size_x,
        1 + step_y : 1 + step_y + size_y,
        1 + step_z : 1 + step_z + size_z,
    ]


def stiffness_padded(padded, mod_pad, fixed_on):
    size_x = padded.shape[-3] - 2
    size_y = padded.shape[-2] - 2
    size_z = padded.shape[-1] - 2
    centre = shifted(padded, 0, 0, 0)
    centre_mod = shifted(mod_pad, 0, 0, 0)
    laplace = jnp.zeros_like(centre)
    for offsets in unit_steps:
        for parity in (1, -1):
            moved_x, moved_y, moved_z = (
                parity * offsets[0],
                parity * offsets[1],
                parity * offsets[2],
            )
            coupling = 0.5 * (centre_mod + shifted(mod_pad, moved_x, moved_y, moved_z))
            laplace = laplace + coupling * (centre - shifted(padded, moved_x, moved_y, moved_z))
    spread = jnp.zeros(padded.shape[:-4] + (size_x + 1, size_y + 1, size_z + 1), jnp.float32)
    for component in range(3):
        offsets = unit_steps[component]
        plane = padded[..., component, :, :, :]
        spread = (
            spread
            + plane[
                ...,
                offsets[0] : offsets[0] + size_x + 1,
                offsets[1] : offsets[1] + size_y + 1,
                offsets[2] : offsets[2] + size_z + 1,
            ]
        )
        spread = spread - plane[..., 0 : size_x + 1, 0 : size_y + 1, 0 : size_z + 1]
    stress = mod_pad[0 : size_x + 1, 0 : size_y + 1, 0 : size_z + 1] * spread
    upper_part = stress[..., 1:, 1:, 1:]
    pieces = []
    for component in range(3):
        offsets = unit_steps[component]
        lower_part = stress[
            ...,
            1 - offsets[0] : 1 - offsets[0] + size_x,
            1 - offsets[1] : 1 - offsets[1] + size_y,
            1 - offsets[2] : 1 - offsets[2] + size_z,
        ]
        pieces.append(lower_part - upper_part)
    grad_div = jnp.stack(pieces, axis=-4)
    return laplace + LAME * grad_div + PENALTY * fixed_on * centre


def diagonal_of(mod_pad, fixed_on):
    centre_mod = shifted(mod_pad, 0, 0, 0)
    total = jnp.zeros_like(centre_mod)
    for offsets in unit_steps:
        for parity in (1, -1):
            total = total + 0.5 * (
                centre_mod
                + shifted(mod_pad, parity * offsets[0], parity * offsets[1], parity * offsets[2])
            )
    pieces = []
    for offsets in unit_steps:
        lower_mod = shifted(mod_pad, -offsets[0], -offsets[1], -offsets[2])
        pieces.append(total + LAME * (centre_mod + lower_mod) + PENALTY * fixed_on)
    return jnp.stack(pieces, axis=0)


def coarse_solve(factor, rhs_vec):
    lower_sol = lax.linalg.triangular_solve(factor, rhs_vec[:, None], left_side=True, lower=True)
    return lax.linalg.triangular_solve(
        factor, lower_sol, left_side=True, lower=True, transpose_a=True
    )[:, 0]


def body(density, fixed_mask, load_mask, forces):
    gx_count = lax.axis_size(GX)
    gy_count = lax.axis_size("gy")
    gz_count = lax.axis_size("gz")
    own_slab = lax.axis_index(GX)
    own_row = lax.axis_index("gy")
    own_col = lax.axis_index("gz")
    size_x, size_y, size_z = density.shape
    modulus_field = modulus(density)
    mod_pad = extended(modulus_field, ((GX, 0), ("gy", 1), ("gz", 2)), 1)
    fixed_on = fixed_mask.astype(jnp.float32)
    diagonal = diagonal_of(mod_pad, fixed_on)
    load_field = forces * (0.25 + load_mask.astype(jnp.float32))[None]

    def stiffness(trial_field):
        padded = with_halo(trial_field, ((GX, 1), ("gy", 2), ("gz", 3)), 1)
        return stiffness_padded(padded, mod_pad, fixed_on)

    def slab_totals(local_vec):
        partial_value = over_copies(local_vec, ("gy", "gz"))
        return collect(partial_value[None], GX, 0)

    x_places = jnp.arange(size_x + 2, dtype=jnp.int32) - 1
    y_places = jnp.arange(size_y + 2, dtype=jnp.int32) - 1
    z_places = jnp.arange(size_z + 2, dtype=jnp.int32) - 1
    slab_of = own_slab + jnp.where(x_places < 0, -1, 0) + jnp.where(x_places >= size_x, 1, 0)
    inside_y = jnp.logical_not(
        (y_places < 0) & (own_row == 0) | (y_places >= size_y) & (own_row == gy_count - 1)
    )
    inside_z = jnp.logical_not(
        (z_places < 0) & (own_col == 0) | (z_places >= size_z) & (own_col == gz_count - 1)
    )
    indicators = []
    for offset in (-1, 0, 1):
        match_x = (slab_of == own_slab + offset) & (slab_of >= 0) & (slab_of < gx_count)
        indicators.append(
            (match_x[:, None, None] & inside_y[None, :, None] & inside_z[None, None, :]).astype(
                jnp.float32
            )
        )
    indicator_stack = jnp.stack(indicators, axis=0)
    identity = jnp.eye(3, dtype=jnp.float32)
    trial_stack = indicator_stack[:, None, None] * identity[None, :, :, None, None, None]
    slab_images = stiffness_padded(trial_stack, mod_pad, fixed_on)
    local_rows = slab_images.sum(axis=(3, 4, 5)).reshape(27)
    block_rows = slab_totals(local_rows).reshape(gx_count, 3, 3, 3)
    row_ids = jnp.arange(gx_count, dtype=jnp.int32)[:, None]
    col_ids = jnp.arange(gx_count, dtype=jnp.int32)[None, :]
    coarse = jnp.zeros((gx_count, 3, gx_count, 3), jnp.float32)
    for offset_id in range(3):
        band_mask = (col_ids - row_ids == offset_id - 1).astype(jnp.float32)
        block_vals = jnp.transpose(block_rows[:, offset_id], (0, 2, 1))
        coarse = coarse + band_mask[:, None, :, None] * block_vals[:, :, None, :]
    factor = jnp.linalg.cholesky(coarse.reshape(3 * gx_count, 3 * gx_count))

    def precondition(residual):
        smooth_one = OMEGA * residual / diagonal
        image_one = stiffness(smooth_one)
        after_one = residual - image_one
        totals = slab_totals(after_one.sum(axis=(1, 2, 3)))
        correction = coarse_solve(factor, totals.reshape(-1)).reshape(gx_count, 3)
        own_value = lax.dynamic_slice_in_dim(correction, own_slab, 1, 0)[0]
        smooth_two = smooth_one + own_value[:, None, None, None]
        padded_corr = jnp.concatenate(
            [jnp.zeros((1, 3), jnp.float32), correction, jnp.zeros((1, 3), jnp.float32)], axis=0
        )
        nearby = lax.dynamic_slice_in_dim(padded_corr, own_slab, 3, 0)
        image_two = image_one + (nearby[:, :, None, None, None, None] * slab_images).sum(
            axis=(0, 1)
        )
        return smooth_two + OMEGA * (residual - image_two) / diagonal

    def dot_pair(residual, precond, applied):
        return (
            by_axis(jnp.sum(residual * precond), GX_GY_GZ),
            by_axis(jnp.sum(precond * applied), GX_GY_GZ),
        )

    solution = jnp.zeros_like(load_field)
    residual = load_field
    precond = precondition(residual)
    applied = stiffness(precond)
    norm_now, curvature_sum = dot_pair(residual, precond, applied)
    step_size = norm_now / curvature_sum
    search = precond
    image_field = applied
    for iteration in range(ITERS):
        solution = solution + step_size * search
        residual = residual - step_size * image_field
        if iteration + 1 < ITERS:
            precond = precondition(residual)
            applied = stiffness(precond)
            norm_next, curvature_sum = dot_pair(residual, precond, applied)
            ratio_next = norm_next / norm_now
            step_size = norm_next / (curvature_sum - ratio_next * norm_next / step_size)
            search = precond + ratio_next * search
            image_field = applied + ratio_next * image_field
            norm_now = norm_next
    return (solution, residual)


def solution(mesh):
    finer = Mesh(
        mesh.devices.reshape(4, 12, mesh.shape["gy"], mesh.shape["gz"]),
        ("gx_0", "gx_1", "gy", "gz"),
    )
    placed = (P(GX, "gy", "gz"), P(GX, "gy", "gz"), P(GX, "gy", "gz"), P(None, GX, "gy", "gz"))
    return jax.shard_map(
        body,
        mesh=finer,
        in_specs=placed,
        out_specs=(P(None, GX, "gy", "gz"), P(None, GX, "gy", "gz")),
        check_vma=False,
    )
```

profile of v0, /device:TPU:1, one launch (start us, length us, event | category | flops | bytes accessed | tf_op | source)
XLA Modules:
  0.0 413.6 jit_solution(11914179961785395279)
XLA Ops:
  7.5 8.9 %collective-permute-start.2 = (f32[4,1,128]{2,1,0:T(1,128)S(1)}, f32[4,1,128]{2,1,0:T(1,128)S(1)}, u32[]{:S(2)}, u32[]{:S(2)}) collective-permute-start(f32[4,1,128]{2,1,0:T(1,128)S(1)} %get-tuple-element.161), channel_id=1, source_target_pairs={{8,0},{9,1},{10,2},{11,3},{12,4},{13,5},{14,6},{15,7},{24,16},{25,... | collective-permute-start | bytes 6152 | tf_op jit(solution)/shard_map/ppermute | solution.py:27
  26.5 4.9 %collective-permute-start.7 = (f32[3,1,16,128]{3,2,1,0:T(8,128)S(1)}, f32[3,1,16,128]{3,2,1,0:T(8,128)S(1)}, u32[]{:S(2)}, u32[]{:S(2)}) collective-permute-start(f32[3,1,16,128]{3,2,1,0:T(8,128)S(1)} %get-tuple-element.151), channel_id=1, source_target_pairs={{0,16},{16,32},{32,48},{48,64},{64,80},{80,96},{96,112},{112,128},... | collective-permute-start | bytes 73736 | tf_op jit(solution)/shard_map/ppermute | solution.py:43
  32.3 5.0 %collective-permute-start.8 = (f32[3,6,1,128]{3,2,1,0:T(1,128)S(1)}, f32[3,6,1,128]{3,2,1,0:T(1,128)S(1)}, u32[]{:S(2)}, u32[]{:S(2)}) collective-permute-start(f32[3,6,1,128]{3,2,1,0:T(1,128)S(1)} %get-tuple-element.132), channel_id=1, source_target_pairs={{8,0},{9,1},{10,2},{11,3},{12,4},{13,5},{14,6},{15,7},{24,16},{25,... | collective-permute-start | bytes 27656 | tf_op jit(solution)/shard_map/ppermute | solution.py:46
  53.8 9.5 %all-to-all-start.2 = ((f32[16,1,3]{2,1,0:T(1,128)}), f32[16,1,3]{2,1,0:T(1,128)S(1)}, u32[]{:S(2)}, u32[]{:S(2)}) async-start(f32[16,1,3]{2,1,0:T(1,128)} %broadcast_in_dim.24), calls=%async_computation.2 | async-start | bytes 16384 | tf_op jit(solution)/shard_map/all_to_all | solution.py:53
  75.5 6.2 %all-to-all-done = f32[16,1,27]{2,1,0:T(1,128)S(1)} async-done(((f32[16,1,27]{2,1,0:T(1,128)}), f32[16,1,27]{2,1,0:T(1,128)S(1)}, u32[]{:S(2)}, u32[]{:S(2)}) %all-to-all-start) | async-done | bytes 1760 | tf_op jit(solution)/shard_map/all_to_all | solution.py:53
  82.4 19.3 %all-to-all-start.3 = ((f32[48,1,3]{2,1,0:T(1,128)}), f32[48,1,3]{2,1,0:T(1,128)S(1)}, u32[]{:S(2)}, u32[]{:S(2)}) async-start(f32[48,1,3]{2,1,0:T(1,128)} %broadcast_in_dim.25), calls=%async_computation.3 | async-start | bytes 49152 | tf_op jit(solution)/shard_map/all_to_all | solution.py:53
  102.4 10.4 %all-to-all-done.3 = f32[48,1,3]{2,1,0:T(1,128)S(1)} async-done(((f32[48,1,3]{2,1,0:T(1,128)}), f32[48,1,3]{2,1,0:T(1,128)S(1)}, u32[]{:S(2)}, u32[]{:S(2)}) %all-to-all-start.3) | async-done | bytes 608 | tf_op jit(solution)/shard_map/all_to_all | solution.py:53
  120.1 9.0 %all-to-all-done.1 = f32[48,1,27]{2,1,0:T(1,128)S(1)} async-done(((f32[48,1,27]{2,1,0:T(1,128)}), f32[48,1,27]{2,1,0:T(1,128)S(1)}, u32[]{:S(2)}, u32[]{:S(2)}) %all-to-all-start.1) | async-done | bytes 5216 | tf_op jit(solution)/shard_map/all_to_all | solution.py:53
  137.5 11.7 %cholesky.51 = f32[128,128]{1,0:T(8,128)S(1)} custom-call(f32[128,128]{1,0:T(8,128)S(1)} %cholesky.124), custom_call_target="Cholesky" | custom-call | tf_op jit(solution)/shard_map/jit(cholesky)/cholesky | solution.py:215
  149.3 9.8 %custom-call.17 = f32[1,128,128]{1,2,0:T(8,128)S(1)} custom-call(f32[1,128,128]{2,1,0:T(8,128)S(1)} %get-tuple-element.154), custom_call_target="InvertDiagBlocksLowerTriangular" | custom-call | tf_op jit(solution)/shard_map/jit(cholesky)/cholesky | solution.py:215
  163.7 19.9 %custom-call.21 = f32[2,128,128]{1,2,0:T(8,128)S(1)} custom-call(f32[2,128,128]{2,1,0:T(8,128)S(1)} %pad_maximum_fusion.8), custom_call_target="InvertDiagBlocksLowerTriangular" | custom-call | tf_op jit(solution)/shard_map/triangular_solve/custom-call.4 | solution.py:157
  191.6 6.3 %collective-permute-start.14 = (f32[3,6,1,128]{3,2,1,0:T(1,128)S(1)}, f32[3,6,1,128]{3,2,1,0:T(1,128)S(1)}, u32[]{:S(2)}, u32[]{:S(2)}) collective-permute-start(f32[3,6,1,128]{3,2,1,0:T(1,128)S(1)} %get-tuple-element.128), channel_id=1, source_target_pairs={{8,0},{9,1},{10,2},{11,3},{12,4},{13,5},{14,6},{15,7},{24,16},{25,... | collective-permute-start | bytes 27656 | tf_op jit(solution)/shard_map/ppermute | solution.py:46
  212.4 11.2 %all-reduce.14 = (f32[]{:T(128)}, f32[]{:T(128)}) all-reduce(f32[]{:T(128)} %get-tuple-element.59, f32[]{:T(128)} %get-tuple-element.58), channel_id=1, replica_groups=mesh['gx_0'=4,'gx_1'=12,'gy'=2,'gz'=8] {'gx_0'}, use_global_device_ids=true, to_apply=%region_10.13 | all-reduce | flops 2 | bytes 16 | tf_op jit(solution)/shard_map/psum | solution.py:72
  223.6 16.1 %all-reduce.10 = (f32[]{:T(128)}, f32[]{:T(128)}) all-reduce(f32[]{:T(128)} %get-tuple-element.70, f32[]{:T(128)} %get-tuple-element.71), channel_id=1, replica_groups=mesh['gx_0'=4,'gx_1'=12,'gy'=2,'gz'=8] {'gx_1'}, use_global_device_ids=true, to_apply=%region_11.14 | all-reduce | flops 2 | bytes 16 | tf_op jit(solution)/shard_map/psum | solution.py:72
  239.8 11.1 %all-reduce.16 = (f32[]{:T(128)}, f32[]{:T(128)}) all-reduce(f32[]{:T(128)} %get-tuple-element.62, f32[]{:T(128)} %get-tuple-element.63), channel_id=1, replica_groups=mesh['gx_0'=4,'gx_1'=12,'gy'=2,'gz'=8] {'gy'}, use_global_device_ids=true, to_apply=%region_12.15 | all-reduce | flops 2 | bytes 16 | tf_op jit(solution)/shard_map/psum | solution.py:72
  250.9 13.5 %all-reduce.12 = (f32[]{:T(128)}, f32[]{:T(128)}) all-reduce(f32[]{:T(128)} %get-tuple-element.74, f32[]{:T(128)} %get-tuple-element.75), channel_id=1, replica_groups=mesh['gx_0'=4,'gx_1'=12,'gy'=2,'gz'=8] {'gz'}, use_global_device_ids=true, to_apply=%region_13.16 | all-reduce | flops 2 | bytes 16 | tf_op jit(solution)/shard_map/psum | solution.py:72
  272.3 6.9 %collective-permute-start.20 = (f32[3,6,1,128]{3,2,1,0:T(1,128)S(1)}, f32[3,6,1,128]{3,2,1,0:T(1,128)S(1)}, u32[]{:S(2)}, u32[]{:S(2)}) collective-permute-start(f32[3,6,1,128]{3,2,1,0:T(1,128)S(1)} %get-tuple-element.126), channel_id=1, source_target_pairs={{8,0},{9,1},{10,2},{11,3},{12,4},{13,5},{14,6},{15,7},{24,16},{25,... | collective-permute-start | bytes 27656 | tf_op jit(solution)/shard_map/ppermute | solution.py:46
  292.9 15.5 %all_to_all.33 = f32[16,1,3]{2,1,0:T(1,128)S(1)} all-to-all(f32[16,1,3]{2,1,0:T(1,128)S(1)} %broadcast_in_dim.26), channel_id=1, replica_groups=mesh['gx_0'=4,'gx_1'=12,'gy'=2,'gz'=8] {'gy','gz'}, dimensions={0} | all-to-all | bytes 384 | tf_op jit(solution)/shard_map/all_to_all | solution.py:53
  308.5 18.8 %all_to_all.34 = f32[48,1,3]{2,1,0:T(1,128)S(1)} all-to-all(f32[48,1,3]{2,1,0:T(1,128)S(1)} %broadcast_in_dim.27), channel_id=1, replica_groups=mesh['gx_0'=4,'gx_1'=12,'gy'=2,'gz'=8] {'gx_0','gx_1'}, dimensions={0} | all-to-all | bytes 1152 | tf_op jit(solution)/shard_map/all_to_all | solution.py:53
  336.1 5.2 %collective-permute-start.26 = (f32[3,6,1,128]{3,2,1,0:T(1,128)S(1)}, f32[3,6,1,128]{3,2,1,0:T(1,128)S(1)}, u32[]{:S(2)}, u32[]{:S(2)}) collective-permute-start(f32[3,6,1,128]{3,2,1,0:T(1,128)S(1)} %get-tuple-element.124), channel_id=1, source_target_pairs={{8,0},{9,1},{10,2},{11,3},{12,4},{13,5},{14,6},{15,7},{24,16},{25,... | collective-permute-start | bytes 27656 | tf_op jit(solution)/shard_map/ppermute | solution.py:46
  355.5 11.3 %all-reduce.13 = (f32[]{:T(128)}, f32[]{:T(128)}) all-reduce(f32[]{:T(128)} %get-tuple-element.57, f32[]{:T(128)} %get-tuple-element.56), channel_id=1, replica_groups=mesh['gx_0'=4,'gx_1'=12,'gy'=2,'gz'=8] {'gx_0'}, use_global_device_ids=true, to_apply=%region_23.26 | all-reduce | flops 2 | bytes 16 | tf_op jit(solution)/shard_map/psum | solution.py:72
  366.8 16.2 %all-reduce.9 = (f32[]{:T(128)}, f32[]{:T(128)}) all-reduce(f32[]{:T(128)} %get-tuple-element.68, f32[]{:T(128)} %get-tuple-element.69), channel_id=1, replica_groups=mesh['gx_0'=4,'gx_1'=12,'gy'=2,'gz'=8] {'gx_1'}, use_global_device_ids=true, to_apply=%region_24.27 | all-reduce | flops 2 | bytes 16 | tf_op jit(solution)/shard_map/psum | solution.py:72
  383.0 11.2 %all-reduce.15 = (f32[]{:T(128)}, f32[]{:T(128)}) all-reduce(f32[]{:T(128)} %get-tuple-element.60, f32[]{:T(128)} %get-tuple-element.61), channel_id=1, replica_groups=mesh['gx_0'=4,'gx_1'=12,'gy'=2,'gz'=8] {'gy'}, use_global_device_ids=true, to_apply=%region_25.28 | all-reduce | flops 2 | bytes 16 | tf_op jit(solution)/shard_map/psum | solution.py:72
  394.3 13.6 %all-reduce.11 = (f32[]{:T(128)}, f32[]{:T(128)}) all-reduce(f32[]{:T(128)} %get-tuple-element.72, f32[]{:T(128)} %get-tuple-element.73), channel_id=1, replica_groups=mesh['gx_0'=4,'gx_1'=12,'gy'=2,'gz'=8] {'gz'}, use_global_device_ids=true, to_apply=%region_26.29 | all-reduce | flops 2 | bytes 16 | tf_op jit(solution)/shard_map/psum | solution.py:72
  (259 shorter events, 132.8 us)
Async XLA Ops:
  1.4 20.2 %collective-permute-start.1 = (f32[1,16,128]{2,1,0:T(8,128)S(1)}, f32[1,16,128]{2,1,0:T(8,128)S(1)}, u32[]{:S(2)}, u32[]{:S(2)}) collective-permute-start(f32[1,16,128]{2,1,0:T(8,128)S(1)} %get-tuple-element.163), channel_id=1, source_target_pairs={{0,16},{16,32},{32,48},{48,64},{64,80},{80,96},{96,112},{112,128},... | collective-permute-start | bytes 24584 | tf_op jit(solution)/shard_map/ppermute | solution.py:26
  6.2 15.4 %collective-permute-start = (f32[1,16,128]{2,1,0:T(8,128)S(1)}, f32[1,16,128]{2,1,0:T(8,128)S(1)}, u32[]{:S(2)}, u32[]{:S(2)}) collective-permute-start(f32[1,16,128]{2,1,0:T(8,128)S(1)} %get-tuple-element.162), channel_id=1, source_target_pairs={{16,0},{32,16},{48,32},{64,48},{80,64},{96,80},{112,96},{128,112},... | collective-permute-start | bytes 24584 | tf_op jit(solution)/shard_map/ppermute | solution.py:27
  7.5 12.7 %collective-permute-start.2 = (f32[4,1,128]{2,1,0:T(1,128)S(1)}, f32[4,1,128]{2,1,0:T(1,128)S(1)}, u32[]{:S(2)}, u32[]{:S(2)}) collective-permute-start(f32[4,1,128]{2,1,0:T(1,128)S(1)} %get-tuple-element.161), channel_id=1, source_target_pairs={{8,0},{9,1},{10,2},{11,3},{12,4},{13,5},{14,6},{15,7},{24,16},{25,... | collective-permute-start | bytes 6152 | tf_op jit(solution)/shard_map/ppermute | solution.py:27
  25.2 6.6 %collective-permute-start.6 = (f32[3,1,16,128]{3,2,1,0:T(8,128)S(1)}, f32[3,1,16,128]{3,2,1,0:T(8,128)S(1)}, u32[]{:S(2)}, u32[]{:S(2)}) collective-permute-start(f32[3,1,16,128]{3,2,1,0:T(8,128)S(1)} %get-tuple-element.152), channel_id=1, source_target_pairs={{16,0},{32,16},{48,32},{64,48},{80,64},{96,80},{112,96},{128,112},... | collective-permute-start | bytes 73736 | tf_op jit(solution)/shard_map/ppermute | solution.py:46
  26.5 5.8 %collective-permute-start.7 = (f32[3,1,16,128]{3,2,1,0:T(8,128)S(1)}, f32[3,1,16,128]{3,2,1,0:T(8,128)S(1)}, u32[]{:S(2)}, u32[]{:S(2)}) collective-permute-start(f32[3,1,16,128]{3,2,1,0:T(8,128)S(1)} %get-tuple-element.151), channel_id=1, source_target_pairs={{0,16},{16,32},{32,48},{48,64},{64,80},{80,96},{96,112},{112,128},... | collective-permute-start | bytes 73736 | tf_op jit(solution)/shard_map/ppermute | solution.py:43
  32.3 6.4 %collective-permute-start.8 = (f32[3,6,1,128]{3,2,1,0:T(1,128)S(1)}, f32[3,6,1,128]{3,2,1,0:T(1,128)S(1)}, u32[]{:S(2)}, u32[]{:S(2)}) collective-permute-start(f32[3,6,1,128]{3,2,1,0:T(1,128)S(1)} %get-tuple-element.132), channel_id=1, source_target_pairs={{8,0},{9,1},{10,2},{11,3},{12,4},{13,5},{14,6},{15,7},{24,16},{25,... | collective-permute-start | bytes 27656 | tf_op jit(solution)/shard_map/ppermute | solution.py:46
  40.6 8.7 %collective-permute-start.10 = (f32[3,6,18,1]{3,2,1,0:T(8,128)S(1)}, f32[3,6,18,1]{3,2,1,0:T(8,128)S(1)}, u32[]{:S(2)}, u32[]{:S(2)}) collective-permute-start(f32[3,6,18,1]{3,2,1,0:T(8,128)S(1)} %get-tuple-element.122), channel_id=1, source_target_pairs={{1,0},{2,1},{3,2},{4,3},{5,4},{6,5},{7,6},{9,8},{10,9},{11,10},{12... | collective-permute-start | bytes 3896 | tf_op jit(solution)/shard_map/ppermute | solution.py:46
  41.9 8.3 %collective-permute-start.11 = (f32[3,6,18,1]{3,2,1,0:T(8,128)S(1)}, f32[3,6,18,1]{3,2,1,0:T(8,128)S(1)}, u32[]{:S(2)}, u32[]{:S(2)}) collective-permute-start(f32[3,6,18,1]{3,2,1,0:T(8,128)S(1)} %get-tuple-element.121), channel_id=1, source_target_pairs={{0,1},{1,2},{2,3},{3,4},{4,5},{5,6},{6,7},{8,9},{9,10},{10,11},{11... | collective-permute-start | bytes 3896 | tf_op jit(solution)/shard_map/ppermute | solution.py:43
  53.8 16.4 %all-to-all-start.2 = ((f32[16,1,3]{2,1,0:T(1,128)}), f32[16,1,3]{2,1,0:T(1,128)S(1)}, u32[]{:S(2)}, u32[]{:S(2)}) async-start(f32[16,1,3]{2,1,0:T(1,128)} %broadcast_in_dim.24), calls=%async_computation.2 | async-start | bytes 16384 | tf_op jit(solution)/shard_map/all_to_all | solution.py:53
  70.9 10.9 %all-to-all-start = ((f32[16,1,27]{2,1,0:T(1,128)}), f32[16,1,27]{2,1,0:T(1,128)S(1)}, u32[]{:S(2)}, u32[]{:S(2)}) async-start(f32[16,1,27]{2,1,0:T(1,128)} %broadcast_in_dim.22), calls=%async_computation | async-start | bytes 16384 | tf_op jit(solution)/shard_map/all_to_all | solution.py:53
  82.4 30.4 %all-to-all-start.3 = ((f32[48,1,3]{2,1,0:T(1,128)}), f32[48,1,3]{2,1,0:T(1,128)S(1)}, u32[]{:S(2)}, u32[]{:S(2)}) async-start(f32[48,1,3]{2,1,0:T(1,128)} %broadcast_in_dim.25), calls=%async_computation.3 | async-start | bytes 49152 | tf_op jit(solution)/shard_map/all_to_all | solution.py:53
  113.4 15.6 %all-to-all-start.1 = ((f32[48,1,27]{2,1,0:T(1,128)}), f32[48,1,27]{2,1,0:T(1,128)S(1)}, u32[]{:S(2)}, u32[]{:S(2)}) async-start(f32[48,1,27]{2,1,0:T(1,128)} %broadcast_in_dim.23), calls=%async_computation.1 | async-start | bytes 49152 | tf_op jit(solution)/shard_map/all_to_all | solution.py:53
  185.3 5.3 %collective-permute-start.12 = (f32[3,1,16,128]{3,2,1,0:T(8,128)S(1)}, f32[3,1,16,128]{3,2,1,0:T(8,128)S(1)}, u32[]{:S(2)}, u32[]{:S(2)}) collective-permute-start(f32[3,1,16,128]{3,2,1,0:T(8,128)S(1)} %get-tuple-element.150), channel_id=1, source_target_pairs={{16,0},{32,16},{48,32},{64,48},{80,64},{96,80},{112,96},{128,112},... | collective-permute-start | bytes 73736 | tf_op jit(solution)/shard_map/ppermute | solution.py:46
  191.6 7.6 %collective-permute-start.14 = (f32[3,6,1,128]{3,2,1,0:T(1,128)S(1)}, f32[3,6,1,128]{3,2,1,0:T(1,128)S(1)}, u32[]{:S(2)}, u32[]{:S(2)}) collective-permute-start(f32[3,6,1,128]{3,2,1,0:T(1,128)S(1)} %get-tuple-element.128), channel_id=1, source_target_pairs={{8,0},{9,1},{10,2},{11,3},{12,4},{13,5},{14,6},{15,7},{24,16},{25,... | collective-permute-start | bytes 27656 | tf_op jit(solution)/shard_map/ppermute | solution.py:46
  201.2 8.7 %collective-permute-start.16 = (f32[3,6,18,1]{3,2,1,0:T(8,128)S(1)}, f32[3,6,18,1]{3,2,1,0:T(8,128)S(1)}, u32[]{:S(2)}, u32[]{:S(2)}) collective-permute-start(f32[3,6,18,1]{3,2,1,0:T(8,128)S(1)} %get-tuple-element.120), channel_id=1, source_target_pairs={{1,0},{2,1},{3,2},{4,3},{5,4},{6,5},{7,6},{9,8},{10,9},{11,10},{12... | collective-permute-start | bytes 3896 | tf_op jit(solution)/shard_map/ppermute | solution.py:46
  202.5 8.4 %collective-permute-start.17 = (f32[3,6,18,1]{3,2,1,0:T(8,128)S(1)}, f32[3,6,18,1]{3,2,1,0:T(8,128)S(1)}, u32[]{:S(2)}, u32[]{:S(2)}) collective-permute-start(f32[3,6,18,1]{3,2,1,0:T(8,128)S(1)} %get-tuple-element.119), channel_id=1, source_target_pairs={{0,1},{1,2},{2,3},{3,4},{4,5},{5,6},{6,7},{8,9},{9,10},{10,11},{11... | collective-permute-start | bytes 3896 | tf_op jit(solution)/shard_map/ppermute | solution.py:43
  265.8 5.6 %collective-permute-start.18 = (f32[3,1,16,128]{3,2,1,0:T(8,128)S(1)}, f32[3,1,16,128]{3,2,1,0:T(8,128)S(1)}, u32[]{:S(2)}, u32[]{:S(2)}) collective-permute-start(f32[3,1,16,128]{3,2,1,0:T(8,128)S(1)} %get-tuple-element.148), channel_id=1, source_target_pairs={{16,0},{32,16},{48,32},{64,48},{80,64},{96,80},{112,96},{128,112},... | collective-permute-start | bytes 73736 | tf_op jit(solution)/shard_map/ppermute | solution.py:46
  272.3 8.2 %collective-permute-start.20 = (f32[3,6,1,128]{3,2,1,0:T(1,128)S(1)}, f32[3,6,1,128]{3,2,1,0:T(1,128)S(1)}, u32[]{:S(2)}, u32[]{:S(2)}) collective-permute-start(f32[3,6,1,128]{3,2,1,0:T(1,128)S(1)} %get-tuple-element.126), channel_id=1, source_target_pairs={{8,0},{9,1},{10,2},{11,3},{12,4},{13,5},{14,6},{15,7},{24,16},{25,... | collective-permute-start | bytes 27656 | tf_op jit(solution)/shard_map/ppermute | solution.py:46
  282.5 8.7 %collective-permute-start.22 = (f32[3,6,18,1]{3,2,1,0:T(8,128)S(1)}, f32[3,6,18,1]{3,2,1,0:T(8,128)S(1)}, u32[]{:S(2)}, u32[]{:S(2)}) collective-permute-start(f32[3,6,18,1]{3,2,1,0:T(8,128)S(1)} %get-tuple-element.118), channel_id=1, source_target_pairs={{1,0},{2,1},{3,2},{4,3},{5,4},{6,5},{7,6},{9,8},{10,9},{11,10},{12... | collective-permute-start | bytes 3896 | tf_op jit(solution)/shard_map/ppermute | solution.py:46
  283.8 8.3 %collective-permute-start.23 = (f32[3,6,18,1]{3,2,1,0:T(8,128)S(1)}, f32[3,6,18,1]{3,2,1,0:T(8,128)S(1)}, u32[]{:S(2)}, u32[]{:S(2)}) collective-permute-start(f32[3,6,18,1]{3,2,1,0:T(8,128)S(1)} %get-tuple-element.117), channel_id=1, source_target_pairs={{0,1},{1,2},{2,3},{3,4},{4,5},{5,6},{6,7},{8,9},{9,10},{10,11},{11... | collective-permute-start | bytes 3896 | tf_op jit(solution)/shard_map/ppermute | solution.py:43
  329.8 5.3 %collective-permute-start.24 = (f32[3,1,16,128]{3,2,1,0:T(8,128)S(1)}, f32[3,1,16,128]{3,2,1,0:T(8,128)S(1)}, u32[]{:S(2)}, u32[]{:S(2)}) collective-permute-start(f32[3,1,16,128]{3,2,1,0:T(8,128)S(1)} %get-tuple-element.146), channel_id=1, source_target_pairs={{16,0},{32,16},{48,32},{64,48},{80,64},{96,80},{112,96},{128,112},... | collective-permute-start | bytes 73736 | tf_op jit(solution)/shard_map/ppermute | solution.py:46
  336.1 6.5 %collective-permute-start.26 = (f32[3,6,1,128]{3,2,1,0:T(1,128)S(1)}, f32[3,6,1,128]{3,2,1,0:T(1,128)S(1)}, u32[]{:S(2)}, u32[]{:S(2)}) collective-permute-start(f32[3,6,1,128]{3,2,1,0:T(1,128)S(1)} %get-tuple-element.124), channel_id=1, source_target_pairs={{8,0},{9,1},{10,2},{11,3},{12,4},{13,5},{14,6},{15,7},{24,16},{25,... | collective-permute-start | bytes 27656 | tf_op jit(solution)/shard_map/ppermute | solution.py:46
  344.5 8.7 %collective-permute-start.28 = (f32[3,6,18,1]{3,2,1,0:T(8,128)S(1)}, f32[3,6,18,1]{3,2,1,0:T(8,128)S(1)}, u32[]{:S(2)}, u32[]{:S(2)}) collective-permute-start(f32[3,6,18,1]{3,2,1,0:T(8,128)S(1)} %get-tuple-element.116), channel_id=1, source_target_pairs={{1,0},{2,1},{3,2},{4,3},{5,4},{6,5},{7,6},{9,8},{10,9},{11,10},{12... | collective-permute-start | bytes 3896 | tf_op jit(solution)/shard_map/ppermute | solution.py:46
  345.8 8.3 %collective-permute-start.29 = (f32[3,6,18,1]{3,2,1,0:T(8,128)S(1)}, f32[3,6,18,1]{3,2,1,0:T(8,128)S(1)}, u32[]{:S(2)}, u32[]{:S(2)}) collective-permute-start(f32[3,6,18,1]{3,2,1,0:T(8,128)S(1)} %get-tuple-element.115), channel_id=1, source_target_pairs={{0,1},{1,2},{2,3},{3,4},{4,5},{5,6},{6,7},{8,9},{9,10},{10,11},{11... | collective-permute-start | bytes 3896 | tf_op jit(solution)/shard_map/ppermute | solution.py:43
  (42 other events, 790.1 us)
where the time goes:
time: 418 us; the launch traced here: 414 us
  blocking collectives  139 us (33%)
  starting transfers between devices  129 us (31%)
  other arithmetic  64.8 us (16%)
  waiting for transfers between devices  59.5 us (14%)
  local copies, waits for them, and re-layouts  11 us (3%)
  between operations  9.12 us (2%)
    psum x8, blocking collectives, by_axis(): x = lax.psum(x, axis)  104 us
    ppermute x12, starting transfers between devices, with_halo(): lax.ppermute(lax.slice_in_dim(block, block.shape[dim] - width, None, axis...  38.4 us
    all_to_all x4, starting transfers between devices, copy_for_each(): return lax.all_to_all(copies, axis, split_axis=0, concat_axis=0, tiled=True)  37.6 us
    all_to_all x2, blocking collectives, copy_for_each(): return lax.all_to_all(copies, axis, split_axis=0, concat_axis=0, tiled=True)  34.4 us
    ppermute x12, starting transfers between devices, with_halo(): lax.ppermute(lax.slice_in_dim(block, 0, width, axis=dim), axis, backward)  33.7 us
    all_to_all x4, waiting for transfers between devices, copy_for_each(): return lax.all_to_all(copies, axis, split_axis=0, concat_axis=0, tiled=True)  30.3 us
    another operation x7, other arithmetic, body(): factor = jnp.linalg.cholesky(coarse.reshape(3 * gx_count, 3 * gx_count))  24.4 us
    another operation x8, other arithmetic, coarse_solve(): lax.linalg.triangular_solve(factor, lower_sol, left_side=True, lower=True...  20.8 us
  transfers between devices with their start and end apart: 34, of which 21 were waited for; matrix products, arithmetic and copies ran while one was open for 2% of the time, Pallas kernels for 0%

commit v1 on v0

v1 whole, which is shorter than its diff:
```python
import jax
import jax.numpy as jnp
from jax import lax
from jax.experimental import pallas as pl
from jax.experimental.pallas import tpu as pltpu
from jax.sharding import PartitionSpec as P

LAME = 0.5
PENALTY = 4.0
OMEGA = 0.5
F32 = jnp.float32
MESH = pl.DeviceIdType.MESH
LANES = 128
N_MSG = 9
N_EX = 5


def steps_for(count):
    steps = 0
    while (1 << steps) < count:
        steps += 1
    return steps


def kernel(
    sizes,
    density,
    fixed_mask,
    load_mask,
    forces,
    disp_out,
    res_out,
    mod_buf,
    fields,
    low_z,
    high_z,
    mod_low,
    pack_send,
    pack_recv,
    edge_recv,
    stress,
    coef,
    dinv_buf,
    keep,
    rows_buf,
    pcr_buf,
    row_send,
    group_recv,
    slab_recv,
    halo_send_sem,
    halo_recv_sem,
    row_send_sem,
    row_recv_sem,
):
    n_gx, n_gy, n_gz = sizes
    n_group = n_gy * n_gz
    gx, gy, gz = (lax.axis_index("gx"), lax.axis_index("gy"), lax.axis_index("gz"))

    def wrap(value, count):
        value = jnp.where(value >= count, value - count, value)
        return jnp.where(value < 0, value + count, value)

    gx_up, gx_dn = (wrap(gx + 1, n_gx), wrap(gx - 1, n_gx))
    gz_up, gz_dn = (wrap(gz + 1, n_gz), wrap(gz - 1, n_gz))
    gy_other = 1 - gy
    gx_side = wrap(gx + 2 * gy - 1, n_gx)
    gz_side = wrap(gz + 2 * gy - 1, n_gz)

    def group_member(step):
        y_at = jnp.where(step >= n_gz, gy_other, gy)
        z_at = wrap(gz + jnp.where(step >= n_gz, step - n_gz, step), n_gz)
        return (gx, y_at, z_at)

    barrier = pltpu.get_barrier_semaphore()

    def greet(where_to):
        pl.semaphore_signal(barrier, inc=1, device_id=where_to, device_id_type=MESH)

    def greet_slab(step, carry):
        greet((wrap(gx + step, n_gx), gy, gz))
        return carry

    def greet_group(step, carry):
        greet(group_member(step))
        return carry

    greet((gx_side, gy_other, gz))
    greet((gx_dn, gy, gz_up))
    greet((gx_up, gy, gz_dn))
    lax.fori_loop(1, n_gx, greet_slab, 0)
    lax.fori_loop(1, n_group, greet_group, 0)

    has_xm = jnp.where(gx > 0, 1.0, 0.0).astype(F32)
    has_xp = jnp.where(gx < n_gx - 1, 1.0, 0.0).astype(F32)
    has_zm = jnp.where(gz > 0, 1.0, 0.0).astype(F32)
    has_zp = jnp.where(gz < n_gz - 1, 1.0, 0.0).astype(F32)
    is_y0 = jnp.where(gy == 0, 1.0, 0.0).astype(F32)
    is_y1 = 1.0 - is_y0

    shape = (4, 16, LANES)
    lane3 = lax.broadcasted_iota(jnp.int32, shape, 2)
    x3 = lax.broadcasted_iota(jnp.int32, shape, 0)
    y3 = lax.broadcasted_iota(jnp.int32, shape, 1)
    slot3 = 2 * x3 + jnp.where(y3 >= 8, 1, 0)
    first_lane, last_lane = (lane3 == 0, lane3 == LANES - 1)
    wide_lane = lax.broadcasted_iota(jnp.int32, (5, 24, LANES), 2) == LANES - 1
    lane2 = lax.broadcasted_iota(jnp.int32, (16, LANES), 1)
    diag2 = lane2 == lax.broadcasted_iota(jnp.int32, (16, LANES), 0)

    zeros_side = jnp.zeros((4, 8, LANES), F32)
    outside = pl.ds(pl.multiple_of(24 * gy, 8), 8)
    for buf, count in [(mod_buf, 1)] + [(fields.at[e], 3) for e in range(N_EX - 1)]:
        for c in range(count):
            buf[c, 1:5, outside, :] = zeros_side

    level = density[...].astype(F32) / 15.0
    mod = 0.05 + 0.95 * level * level * level
    mod_buf[0, 1:5, 8:24, :] = mod
    fixed4 = PENALTY * fixed_mask[...].astype(F32)
    load_scale = 0.25 + load_mask[...].astype(F32)
    load = [forces[c] * load_scale for c in range(3)]

    def pack_side(values, lane):
        total = None
        for c, value in enumerate(values):
            spread = jnp.broadcast_to(value[:, :, lane : lane + 1], shape)
            chosen = jnp.where(lane3 == slot3 + 8 * c, spread, 0.0)
            flat = chosen[0] + chosen[1] + chosen[2] + chosen[3]
            part = flat[0:8] + flat[8:16]
            total = part if total is None else total + part
        return total

    def remote(e, k, src, dst, where_to):
        copy = pltpu.make_async_remote_copy(
            src_ref=src,
            dst_ref=dst,
            send_sem=halo_send_sem.at[e, k],
            recv_sem=halo_recv_sem.at[e, k],
            device_id=where_to,
            device_id_type=MESH,
        )
        copy.start()
        return copy

    def start_halo(e, buf, values, with_edges):
        copies = [
            remote(e, 0, buf.at[:, 4, 8:24, :], buf.at[:, 0, 8:24, :], (gx_up, gy, gz)),
            remote(e, 1, buf.at[:, 1, 8:24, :], buf.at[:, 5, 8:24, :], (gx_dn, gy, gz)),
        ]
        pack_send[e, 0] = pack_side(values, LANES - 1)
        pack_send[e, 1] = pack_side(values, 0)
        copies.append(
            remote(e, 2, pack_send.at[e, 0], pack_recv.at[e, 0], (gx, gy, gz_up))
        )
        copies.append(
            remote(e, 3, pack_send.at[e, 1], pack_recv.at[e, 1], (gx, gy, gz_dn))
        )
        if with_edges:
            copies.append(
                remote(e, 4, pack_send.at[e, 0], pack_recv.at[e, 2], (gx_dn, gy, gz_up))
            )
            copies.append(
                remote(e, 5, pack_send.at[e, 1], pack_recv.at[e, 3], (gx_up, gy, gz_dn))
            )
            copies.append(
                remote(
                    e, 6, pack_send.at[e, 1 - gy], pack_recv.at[e, 4], (gx, gy_other, gz_side)
                )
            )
            copies.append(
                remote(
                    e,
                    7,
                    buf.at[gy, 1 + 3 * gy, pl.ds(pl.multiple_of(16 - 8 * gy, 8), 8), :],
                    edge_recv.at[e],
                    (gx_side, gy_other, gz),
                )
            )
        copies.append(
            remote(
                e,
                8,
                buf.at[:, 1:5, pl.ds(pl.multiple_of(16 - 8 * gy, 8), 8), :],
                buf.at[:, 1:5, pl.ds(pl.multiple_of(24 * gy, 8), 8), :],
                (gx, gy_other, gz),
            )
        )
        return copies

    def finish_halo(e, buf, copies, with_edges):
        for copy in copies:
            copy.wait()
        count = buf.shape[0]
        for c in range(count):
            buf[c, 0, 8:24, :] = buf[c, 0, 8:24, :] * has_xm
            buf[c, 5, 8:24, :] = buf[c, 5, 8:24, :] * has_xp
        low = pack_recv[e, 0] * has_zm
        high = pack_recv[e, 1] * has_zp
        target_low = low_z if with_edges else mod_low
        target_high = high_z
        for c in range(count):
            for x in range(4):
                for t in range(2):
                    j = 8 * c + 2 * x + t
                    rows = slice(8 + 8 * t, 16 + 8 * t)
                    target_low[c, 1 + x, rows, :] = jnp.broadcast_to(low[:, j : j + 1], (8, LANES))
                    target_high[c, 1 + x, rows, :] = jnp.broadcast_to(
                        high[:, j : j + 1], (8, LANES)
                    )
        if with_edges:
            low_x = pack_recv[e, 2] * (has_xp * has_zm)
            high_x = pack_recv[e, 3] * (has_xm * has_zp)
            side = pack_recv[e, 4]
            low_y = side * (is_y0 * has_zm)
            high_y = side * (is_y1 * has_zp)
            for t in range(2):
                rows = slice(8 + 8 * t, 16 + 8 * t)
                j = t
                low_z[0, 5, rows, :] = jnp.broadcast_to(low_x[:, j : j + 1], (8, LANES))
                j = 8 * 2 + 2 * 3 + t
                high_z[2, 0, rows, :] = jnp.broadcast_to(high_x[:, j : j + 1], (8, LANES))
            for x in range(4):
                j = 8 + 2 * x
                low_z[1, 1 + x, 24:32, :] = jnp.broadcast_to(low_y[:, j : j + 1], (8, LANES))
                j = 8 * 2 + 2 * x + 1
                high_z[2, 1 + x, 0:8, :] = jnp.broadcast_to(high_y[:, j : j + 1], (8, LANES))
            corner = edge_recv[e]
            buf[1, 0, 24:32, :] = corner * (is_y0 * has_xm)
            buf[0, 5, 0:8, :] = corner * (is_y1 * has_xp)

    def before(value, low):
        return jnp.where(first_lane, low, pltpu.roll(value, 1, 2))

    def after(value, high):
        return jnp.where(last_lane, high, pltpu.roll(value, LANES - 1, 2))

    def set_field(e, values):
        for c in range(3):
            fields[e, c, 1:5, 8:24, :] = values[c]

    def stiffness(e):
        buf = fields.at[e]
        u_z = buf[2, 0:5, 0:24, :]
        up_z = jnp.where(wide_lane, high_z[2, 0:5, 0:24, :], pltpu.roll(u_z, LANES - 1, 2))
        spread = (
            (buf[0, 1:6, 0:24, :] - buf[0, 0:5, 0:24, :])
            + (buf[1, 0:5, 1:25, :] - buf[1, 0:5, 0:24, :])
            + (up_z - u_z)
        )
        stress[...] = mod_buf[0, 0:5, 0:24, :] * spread
        here = stress[1:5, 8:24, :]
        spread_low = (
            (low_z[0, 2:6, 8:24, :] - low_z[0, 1:5, 8:24, :])
            + (low_z[1, 1:5, 9:25, :] - low_z[1, 1:5, 8:24, :])
            + (buf[2, 1:5, 8:24, :] - low_z[2, 1:5, 8:24, :])
        )
        below = [
            stress[0:4, 8:24, :],
            stress[1:5, 7:23, :],
            before(here, mod_low[0, 1:5, 8:24, :] * spread_low),
        ]
        images = []
        for c in range(3):
            centre = buf[c, 1:5, 8:24, :]
            image = coef[6] * centre
            image = image - coef[0] * buf[c, 0:4, 8:24, :]
            image = image - coef[1] * buf[c, 2:6, 8:24, :]
            image = image - coef[2] * buf[c, 1:5, 7:23, :]
            image = image - coef[3] * buf[c, 1:5, 9:25, :]
            image = image - coef[4] * before(centre, low_z[c, 1:5, 8:24, :])
            image = image - coef[5] * after(centre, high_z[c, 1:5, 8:24, :])
            images.append(image + LAME * (below[c] - here))
        return images

    def put_sum(q, value):
        if value.ndim == 3:
            value = value[0] + value[1] + value[2] + value[3]
        value = value[0:8] + value[8:16]
        rows_buf[q : q + 1, :] = jnp.sum(value, axis=0, keepdims=True)

    def make_row():
        sums = jnp.sum(rows_buf[...], axis=1, keepdims=True)
        return jnp.sum(jnp.where(diag2, sums, 0.0), axis=0, keepdims=True)

    me_group = gy * n_gz + gz

    def gather_rows(i, row):
        row_send[i, 0] = row
        group_recv[i, me_group] = row

        def group_copy(step):
            return pltpu.make_async_remote_copy(
                src_ref=row_send.at[i, 0],
                dst_ref=group_recv.at[i, me_group],
                send_sem=row_send_sem.at[i, 0],
                recv_sem=row_recv_sem.at[i, 0],
                device_id=group_member(step),
                device_id_type=MESH,
            )

        def start_group(step, carry):
            group_copy(step).start()
            return carry

        lax.fori_loop(1, n_group, start_group, 0)
        most = group_recv.at[i, pl.ds(0, n_group - 1)]
        pltpu.make_async_copy(most, most, row_recv_sem.at[i, 0]).wait()
        total = group_recv[i, 0]
        for k in range(1, n_group):
            total = total + group_recv[i, k]
        row_send[i, 1] = total
        slab_recv[i, gx] = total

        def start_slab(step, carry):
            pltpu.make_async_remote_copy(
                src_ref=row_send.at[i, 1],
                dst_ref=slab_recv.at[i, gx],
                send_sem=row_send_sem.at[i, 1],
                recv_sem=row_recv_sem.at[i, 1],
                device_id=(wrap(gx + step, n_gx), gy, gz),
                device_id_type=MESH,
            ).start()
            return carry

        lax.fori_loop(1, n_gx, start_slab, 0)
        rest = slab_recv.at[i, pl.ds(0, n_gx - 1)]
        pltpu.make_async_copy(rest, rest, row_recv_sem.at[i, 1]).wait()
        pltpu.make_async_copy(most, most, row_send_sem.at[i, 0]).wait()
        pltpu.make_async_copy(rest, rest, row_send_sem.at[i, 1]).wait()

    def slab_rows(i):
        table = jnp.concatenate(
            [slab_recv[i, k] for k in range(n_gx)]
            + [jnp.zeros((LANES - n_gx, LANES), F32)],
            axis=0,
        )
        return jnp.transpose(table)

    lane_row = lax.broadcasted_iota(jnp.int32, (1, LANES), 1)
    sub8 = lax.broadcasted_iota(jnp.int32, (8, LANES), 0)
    n_steps = steps_for(n_gx)

    def stack3(a, b, c):
        return jnp.where(sub8 == 0, a, jnp.where(sub8 == 1, b, jnp.where(sub8 == 2, c, 0.0)))

    def times(matrix, column):
        return (
            matrix[0] * column[0:1, :] + matrix[1] * column[1:2, :] + matrix[2] * column[2:3, :]
        )

    def inverse(cols):
        a, d, g = (cols[0][0:1, :], cols[0][1:2, :], cols[0][2:3, :])
        b, e, h = (cols[1][0:1, :], cols[1][1:2, :], cols[1][2:3, :])
        c, f, i = (cols[2][0:1, :], cols[2][1:2, :], cols[2][2:3, :])
        m00, m01, m02 = (e * i - f * h, c * h - b * i, b * f - c * e)
        m10, m11, m12 = (f * g - d * i, a * i - c * g, c * d - a * f)
        m20, m21, m22 = (d * h - e * g, b * g - a * h, a * e - b * d)
        scale = 1.0 / (a * m00 + b * m10 + c * m20)
        return [
            stack3(m00 * scale, m10 * scale, m20 * scale),
            stack3(m01 * scale, m11 * scale, m21 * scale),
            stack3(m02 * scale, m12 * scale, m22 * scale),
        ]

    def factorise(lower, main, upper, rhs):
        def body(step, carry):
            stride, low, mid, high, vec = carry
            back = LANES - stride
            inv = inverse(mid)
            inv_dn = [pltpu.roll(v, stride, 1) for v in inv]
            inv_up = [pltpu.roll(v, back, 1) for v in inv]
            alpha = [-times(low, v) for v in inv_dn]
            gamma = [-times(high, v) for v in inv_up]
            for k in range(3):
                pcr_buf[step, k] = alpha[k]
                pcr_buf[step, 3 + k] = gamma[k]
            low_dn = [pltpu.roll(v, stride, 1) for v in low]
            high_dn = [pltpu.roll(v, stride, 1) for v in high]
            low_up = [pltpu.roll(v, back, 1) for v in low]
            high_up = [pltpu.roll(v, back, 1) for v in high]
            vec_dn = pltpu.roll(vec, stride, 1)
            vec_up = pltpu.roll(vec, back, 1)
            new_mid = [
                mid[k] + times(alpha, high_dn[k]) + times(gamma, low_up[k]) for k in range(3)
            ]
            new_low = [times(alpha, v) for v in low_dn]
            new_high = [times(gamma, v) for v in high_up]
            new_vec = vec + times(alpha, vec_dn) + times(gamma, vec_up)
            return (stride * 2, new_low, new_mid, new_high, new_vec)

        _, _, mid, _, vec = lax.fori_loop(
            0, n_steps, body, (jnp.int32(1), lower, main, upper, rhs)
        )
        inv = inverse(mid)
        for k in range(3):
            pcr_buf[n_steps, k] = inv[k]
        return times(inv, vec)

    def solve_again(vec):
        stride = 1
        for step in range(n_steps):
            alpha = [pcr_buf[step, k] for k in range(3)]
            gamma = [pcr_buf[step, 3 + k] for k in range(3)]
            vec_dn = pltpu.roll(vec, stride, 1)
            vec_up = pltpu.roll(vec, LANES - stride, 1)
            vec = vec + times(alpha, vec_dn) + times(gamma, vec_up)
            stride *= 2
        return times([pcr_buf[n_steps, k] for k in range(3)], vec)

    def nearby(solved):
        turned = pltpu.roll(solved, wrap(1 - gx, LANES), 1)
        return [
            [jnp.broadcast_to(turned[c : c + 1, b : b + 1], (16, LANES)) for c in range(3)]
            for b in range(3)
        ]

    pl.semaphore_wait(barrier, n_gx - 1 + n_group - 1 + 3)

    copies = start_halo(0, mod_buf, [mod], False)
    finish_halo(0, mod_buf, copies, False)
    mod_zm = before(mod, mod_low[0, 1:5, 8:24, :])
    mod_zp = after(mod, high_z[0, 1:5, 8:24, :])
    mod_xm, mod_xp = (mod_buf[0, 0:4, 8:24, :], mod_buf[0, 2:6, 8:24, :])
    mod_ym, mod_yp = (mod_buf[0, 1:5, 7:23, :], mod_buf[0, 1:5, 9:25, :])
    couplings = [0.5 * (mod + v) for v in (mod_xm, mod_xp, mod_ym, mod_yp, mod_zm, mod_zp)]
    total = fixed4
    for k in range(6):
        coef[k] = couplings[k]
        total = total + couplings[k]
    coef[6] = total
    for c in range(3):
        dinv_buf[c] = OMEGA / (total + couplings[2 * c])

    first = [load[c] * dinv_buf[c] for c in range(3)]
    set_field(0, first)
    copies = start_halo(1, fields.at[0], first, True)

    low_y_edge = jnp.where(y3 == 0, is_y0, 0.0)
    high_y_edge = jnp.where(y3 == 15, is_y1, 0.0)
    low_z_edge = jnp.where(first_lane, 1.0 - has_zm, 0.0)
    high_z_edge = jnp.where(last_lane, 1.0 - has_zp, 0.0)
    first_x = jnp.where(x3 == 0, 1.0, 0.0)
    last_x = jnp.where(x3 == 3, 1.0, 0.0)
    bound = (
        fixed4
        + couplings[2] * low_y_edge
        + couplings[3] * high_y_edge
        + couplings[4] * low_z_edge
        + couplings[5] * high_z_edge
        + couplings[0] * first_x
        + couplings[1] * last_x
    )
    half = LAME * mod
    half_xm = LAME * mod_xm
    keep[0] = bound
    rows_buf[...] = jnp.zeros((16, LANES), F32)
    put_sum(0, bound + half_xm * first_x + half * last_x)
    put_sum(1, bound + half * high_y_edge)
    put_sum(2, bound + half * high_z_edge)
    put_sum(3, half[3] * high_y_edge[3])
    put_sum(4, half[3] * high_z_edge[3])
    put_sum(5, half * high_y_edge * high_z_edge)
    put_sum(6, couplings[1][3])
    put_sum(7, couplings[1][3] + half[3])

    def image_of(coarse):
        under, own, over = coarse
        bound = keep[0]
        mod = mod_buf[0, 1:5, 8:24, :]
        half = LAME * mod
        half_xm = LAME * mod_buf[0, 0:4, 8:24, :]
        half_ym = LAME * mod_buf[0, 1:5, 7:23, :]
        half_zm = LAME * before(mod, mod_low[0, 1:5, 8:24, :])
        low_x, high_x = (coef[0], coef[1])
        inner_xm = half_xm * (1.0 - first_x)
        down_y, down_z = (half - half_ym, half - half_zm)
        image_x = (
            (bound + half_xm * first_x + half * last_x) * own[0]
            + (half - inner_xm) * (high_y_edge * own[1] + high_z_edge * own[2])
            - first_x
            * (
                (low_x + half_xm) * under[0]
                + half_xm * (high_y_edge * under[1] + high_z_edge * under[2])
            )
            - last_x * (high_x + half) * over[0]
        )
        image_y = (
            (bound + half * high_y_edge) * own[1]
            + down_y * (last_x * (own[0] - over[0]) + high_z_edge * own[2])
            - first_x * low_x * under[1]
            - last_x * high_x * over[1]
        )
        image_z = (
            (bound + half * high_z_edge) * own[2]
            + down_z * (last_x * (own[0] - over[0]) + high_y_edge * own[1])
            - first_x * low_x * under[2]
            - last_x * high_x * over[2]
        )
        return [image_x, image_y, image_z]

    finish_halo(1, fields.at[0], copies, True)
    image_first = stiffness(0)
    rest = [load[c] - image_first[c] for c in range(3)]
    for c in range(3):
        put_sum(8 + c, rest[c])
        keep[1 + c] = rest[c]
    gather_rows(0, make_row())

    table = slab_rows(0)
    real = lane_row < n_gx
    row = [jnp.where(real, table[q : q + 1, :], 0.0) for q in range(11)]
    one = jnp.where(real, 0.0, 1.0)
    none = jnp.zeros((1, LANES), F32)
    main = [
        stack3(row[0] + one, row[3], row[4]),
        stack3(row[3], row[1] + one, row[5]),
        stack3(row[4], row[5], row[2] + one),
    ]
    joined = lane_row < n_gx - 1
    side = [jnp.where(joined, row[q], 0.0) for q in (7, 3, 4, 6)]
    upper = [
        stack3(-side[0], -side[1], -side[2]),
        stack3(none, -side[3], none),
        stack3(none, none, -side[3]),
    ]
    moved = [pltpu.roll(jnp.broadcast_to(v, (8, LANES)), 1, 1)[0:1, :] for v in side]
    lower = [
        stack3(-moved[0], none, none),
        stack3(-moved[1], -moved[3], none),
        stack3(-moved[2], none, -moved[3]),
    ]
    near = nearby(factorise(lower, main, upper, stack3(row[8], row[9], row[10])))
    coarse_image = image_of(near)
    precond = []
    for c in range(3):
        second = fields[0, c, 1:5, 8:24, :] + near[1][c]
        precond.append(second + dinv_buf[c] * (keep[1 + c] - coarse_image[c]))
    set_field(1, precond)
    copies = start_halo(2, fields.at[1], precond, True)
    load = [forces[c] * load_scale for c in range(3)]
    rows_buf[...] = jnp.zeros((16, LANES), F32)
    put_sum(0, load[0] * precond[0] + load[1] * precond[1] + load[2] * precond[2])
    finish_halo(2, fields.at[1], copies, True)
    image = stiffness(1)
    smooth = []
    for c in range(3):
        keep[4 + c] = image[c]
        smooth.append(dinv_buf[c] * image[c])
    set_field(2, smooth)
    copies = start_halo(3, fields.at[2], smooth, True)
    precond = [fields[1, c, 1:5, 8:24, :] for c in range(3)]
    put_sum(1, image[0] * precond[0] + image[1] * precond[1] + image[2] * precond[2])
    finish_halo(3, fields.at[2], copies, True)
    image_smooth = stiffness(2)
    for c in range(3):
        remain = keep[4 + c] - image_smooth[c]
        keep[1 + c] = remain
        put_sum(2 + c, remain)
    gather_rows(1, make_row())

    table = slab_rows(1)
    row = [jnp.where(real, table[q : q + 1, :], 0.0) for q in range(5)]
    norm_now = jnp.sum(row[0], axis=1, keepdims=True)
    curve = jnp.sum(row[1], axis=1, keepdims=True)
    step0 = norm_now / curve
    near = nearby(solve_again(stack3(row[2], row[3], row[4])))
    coarse_image = image_of(near)
    wide0 = jnp.broadcast_to(step0, (16, LANES))
    following = []
    for c in range(3):
        second = fields[2, c, 1:5, 8:24, :] + near[1][c]
        change = second + dinv_buf[c] * (keep[1 + c] - coarse_image[c])
        following.append(fields[1, c, 1:5, 8:24, :] - wide0 * change)
    set_field(3, following)
    copies = start_halo(4, fields.at[3], following, True)
    rows_buf[...] = jnp.zeros((16, LANES), F32)
    residual = []
    product = jnp.zeros(shape, F32)
    for c in range(3):
        residual.append(forces[c] * load_scale - wide0 * keep[4 + c])
        product = product + residual[c] * following[c]
        keep[1 + c] = residual[c]
    put_sum(0, product)
    finish_halo(4, fields.at[3], copies, True)
    image_next = stiffness(3)
    product = jnp.zeros(shape, F32)
    for c in range(3):
        product = product + image_next[c] * fields[3, c, 1:5, 8:24, :]
        keep[7 + c] = image_next[c]
    put_sum(1, product)
    gather_rows(2, make_row())

    both = slab_recv[2, 0]
    for k in range(1, n_gx):
        both = both + slab_recv[2, k]
    norm_next, curve_next = (both[0:1, 0:1], both[0:1, 1:2])
    ratio = norm_next / norm_now
    step1 = norm_next / (curve_next - ratio * norm_next / step0)
    wide_ratio = jnp.broadcast_to(ratio, (16, LANES))
    wide1 = jnp.broadcast_to(step1, (16, LANES))
    for c in range(3):
        previous = fields[1, c, 1:5, 8:24, :]
        search = fields[3, c, 1:5, 8:24, :] + wide_ratio * previous
        disp_out[c] = wide0 * previous + wide1 * search
        res_out[c] = keep[1 + c] - wide1 * (keep[7 + c] + wide_ratio * keep[4 + c])


def solution(mesh):
    sizes = tuple(mesh.shape[name] for name in ("gx", "gy", "gz"))
    n_gx, n_gy, n_gz = sizes
    n_group = n_gy * n_gz
    block = jax.ShapeDtypeStruct((3, 4, 16, LANES), F32)
    vmem = pl.BlockSpec(memory_space=pltpu.VMEM)

    def body(density, fixed_mask, load_mask, forces):
        def run(*refs):
            kernel(sizes, *refs)

        return pl.pallas_call(
            run,
            out_shape=(block, block),
            in_specs=[vmem] * 4,
            out_specs=(vmem, vmem),
            scratch_shapes=[
                pltpu.VMEM((1, 6, 32, LANES), F32),
                pltpu.VMEM((N_EX - 1, 3, 6, 32, LANES), F32),
                pltpu.VMEM((3, 6, 32, LANES), F32),
                pltpu.VMEM((3, 6, 32, LANES), F32),
                pltpu.VMEM((1, 6, 32, LANES), F32),
                pltpu.VMEM((N_EX, 2, 8, LANES), F32),
                pltpu.VMEM((N_EX, 5, 8, LANES), F32),
                pltpu.VMEM((N_EX, 8, LANES), F32),
                pltpu.VMEM((5, 24, LANES), F32),
                pltpu.VMEM((7, 4, 16, LANES), F32),
                pltpu.VMEM((3, 4, 16, LANES), F32),
                pltpu.VMEM((10, 4, 16, LANES), F32),
                pltpu.VMEM((16, LANES), F32),
                pltpu.VMEM((steps_for(n_gx) + 1, 6, 8, LANES), F32),
                pltpu.VMEM((3, 2, 1, LANES), F32),
                pltpu.VMEM((3, n_group, 1, LANES), F32),
                pltpu.VMEM((3, n_gx, 1, LANES), F32),
                pltpu.SemaphoreType.DMA((N_EX, N_MSG)),
                pltpu.SemaphoreType.DMA((N_EX, N_MSG)),
                pltpu.SemaphoreType.DMA((3, 2)),
                pltpu.SemaphoreType.DMA((3, 2)),
            ],
            compiler_params=pltpu.CompilerParams(collective_id=0, has_side_effects=True),
        )(density, fixed_mask, load_mask, forces)

    spec = P("gx", "gy", "gz")
    wide = P(None, "gx", "gy", "gz")
    return jax.shard_map(
        body,
        mesh=mesh,
        in_specs=(spec, spec, spec, wide),
        out_specs=(wide, wide),
        check_vma=False,
    )
```

time: 418 us -> 87.7 us (0.21)
  blocking collectives: 139 us -> 0 us
  starting transfers between devices: 129 us -> 0 us
  Pallas kernels: 0 us -> 84.6 us
  other arithmetic: 64.8 us -> 0 us
  waiting for transfers between devices: 59.5 us -> 0 us
  local copies, waits for them, and re-layouts: 11 us -> 2.22 us
  between operations: 9.12 us -> 0.65 us
    psum x8 -> x0, blocking collectives: 104 us -> none  [by_axis(): x = lax.psum(x, axis)]
    ppermute x30 -> x0, starting transfers between devices: 91 us -> none  [the longest x12 38.4 us: with_halo(): lax.ppermute(lax.slice_in_dim(block, block.shape[dim] - width, None, axis...]
    pallas_call x0 -> x1, Pallas kernels: none -> 84.6 us  [body(): pl.pallas_call(run, out_shape=(block, block), in_specs=[vmem] * 4, out_sp...]
    another operation x23 -> x0, other arithmetic: 46.6 us -> none  [the longest x7 24.4 us: body(): factor = jnp.linalg.cholesky(coarse.reshape(3 * gx_count, 3 * gx_count))]
    all_to_all x4 -> x0, starting transfers between devices: 37.6 us -> none  [copy_for_each(): return lax.all_to_all(copies, axis, split_axis=0, concat_axis=0, tiled=True)]
    all_to_all x2 -> x0, blocking collectives: 34.4 us -> none  [copy_for_each(): return lax.all_to_all(copies, axis, split_axis=0, concat_axis=0, tiled=True)]
    all_to_all x4 -> x0, waiting for transfers between devices: 30.3 us -> none  [copy_for_each(): return lax.all_to_all(copies, axis, split_axis=0, concat_axis=0, tiled=True)]
    ppermute x30 -> x0, waiting for transfers between devices: 29.2 us -> none  [the longest x12 14.1 us: with_halo(): lax.ppermute(lax.slice_in_dim(block, block.shape[dim] - width, None, axis...]
  transfers between devices with their start and end apart: 34 -> 0, of which waited for: 21 -> 0; matrix products, arithmetic and copies ran while one was open for 2% -> 0% of each run, Pallas kernels for 0% -> 0%
where the time goes in v1:
time: 87.7 us; the launch traced here: 87.5 us
  Pallas kernels  84.6 us (96%)
  local copies, waits for them, and re-layouts  2.22 us (3%)
    pallas_call x1, Pallas kernels, body(): pl.pallas_call(run, out_shape=(block, block), in_specs=[vmem] * 4, out_sp...  84.6 us
    unnamed x4, local copies, waits for them, and re-layouts  2.22 us

profile of v1, /device:TPU:1, one launch (start us, length us, event | category | flops | bytes accessed | tf_op | source)
XLA Modules:
  0.0 87.5 jit_solution(10354573908947137176)
XLA Ops:
  0.6 84.6 %shard_map.59 = (f32[3,4,16,128]{3,2,1,0:T(8,128)}, f32[3,4,16,128]{3,2,1,0:T(8,128)}) custom-call(s32[4,16,128]{2,1,0:T(8,128)} %refs_0_.1, s32[4,16,128]{2,1,0:T(8,128)} %refs_1_.1, s32[4,16,128]{2,1,0:T(8,128)} %refs_2_.1, f32[3,4,16,128]{3,2,1,0:T(8,128)} %refs_3_.1), custom_call_target="tpu_custom_call" | custom-call | tf_op jit(solution)/shard_map/pallas_call | solution.py:619
  85.2 0.0 copy-start
  85.3 1.6 %copy.8 = f32[3,4,16,128]{3,2,1,0:T(8,128)} copy(f32[3,4,16,128]{3,2,1,0:T(8,128)} %get-tuple-element.4) | data formatting | bytes 196608
  86.8 0.0 copy-done
  86.8 0.6 copy.9
Async XLA Ops:
  85.2 1.6 %copy-start = (f32[3,4,16,128]{3,2,1,0:T(8,128)S(1)}, f32[3,4,16,128]{3,2,1,0:T(8,128)}, u32[]{:S(2)}) copy-start(f32[3,4,16,128]{3,2,1,0:T(8,128)} %get-tuple-element.5) | copy-start | bytes 294916

commit v2 on v1

--- a/solution.py
+++ b/solution.py
@@ -12,7 +12,9 @@
 MESH = pl.DeviceIdType.MESH
 LANES = 128
 N_MSG = 9
-N_EX = 5
+N_EX = 6
+N_FIELD = 4
+N_BASIS = 10
 
 
 def steps_for(count):
@@ -32,12 +34,17 @@
     res_out,
     mod_buf,
     fields,
-    low_z,
-    high_z,
+    low_all,
+    high_all,
     mod_low,
+    mod_high,
+    basis,
+    basis_low,
+    basis_high,
     pack_send,
     pack_recv,
     edge_recv,
+    basis_edge,
     stress,
     coef,
     dinv_buf,
@@ -47,10 +54,16 @@
     row_send,
     group_recv,
     slab_recv,
+    in_density,
+    in_fixed,
+    in_load,
+    in_forces,
+    in_sem,
     halo_send_sem,
     halo_recv_sem,
     row_send_sem,
     row_recv_sem,
+    flood_sem,
 ):
     n_gx, n_gy, n_gz = sizes
     n_group = n_gy * n_gz
@@ -76,19 +89,54 @@
     def greet(where_to):
         pl.semaphore_signal(barrier, inc=1, device_id=where_to, device_id_type=MESH)
 
-    def greet_slab(step, carry):
-        greet((wrap(gx + step, n_gx), gy, gz))
-        return carry
-
-    def greet_group(step, carry):
-        greet(group_member(step))
-        return carry
-
-    greet((gx_side, gy_other, gz))
-    greet((gx_dn, gy, gz_up))
-    greet((gx_up, gy, gz_dn))
-    lax.fori_loop(1, n_gx, greet_slab, 0)
-    lax.fori_loop(1, n_group, greet_group, 0)
+    near = [
+        (gx_up, gy, gz),
+        (gx_dn, gy, gz),
+        (gx, gy, gz_up),
+        (gx, gy, gz_dn),
+        (gx, gy_other, gz),
+        (gx_side, gy_other, gz),
+        (gx_dn, gy, gz_up),
+        (gx_up, gy, gz_dn),
+        (gx, gy_other, gz_side),
+    ]
+    n_fast = 12 if n_gx == 48 else n_gx
+    n_slow = n_gx // n_fast
+    slow = gx // n_fast
+    fast = gx - slow * n_fast
+    ring_fast = [slow * n_fast + wrap(fast + d, n_fast) for d in (1, -1)]
+    ring_slow = [wrap(slow + d, n_slow) * n_fast + fast for d in (1, -1)]
+    if n_slow > 1:
+        near = near + [(v, gy, gz) for v in ring_slow + ring_fast]
+    for where_to in near:
+        greet(where_to)
+    fetches = []
+    for k, (src, dst) in enumerate(
+        ((density, in_density), (fixed_mask, in_fixed), (load_mask, in_load), (forces, in_forces))
+    ):
+        fetch = pltpu.make_async_copy(src, dst, in_sem.at[k])
+        fetch.start()
+        fetches.append(fetch)
+
+    ring_y = [(gx, gy, gz_up), (gx, gy, gz_dn)]
+    ring_z = [(v, gy, gz) for v in ring_fast]
+    ring_x = [(v, gy, gz) for v in ring_slow]
+    n_y, n_z = (max(n_gz // 2 - 1, 0), max(n_fast // 2 - 1, 0))
+    floods = []
+    for k in range(max(n_y, n_z)):
+        floods.append(([ring_y] if k < n_y else []) + ([ring_z] if k < n_z else []))
+    if n_slow > 1:
+        floods += [[ring_x]] * max(n_slow // 2, 1)
+
+    def flood(first, last):
+        for k in range(first, min(last, len(floods))):
+            for r, ring in enumerate(floods[k]):
+                for where_to in ring:
+                    pl.semaphore_signal(
+                        flood_sem.at[k, r], inc=1, device_id=where_to, device_id_type=MESH
+                    )
+            for r in range(len(floods[k])):
+                pl.semaphore_wait(flood_sem.at[k, r], 2)
 
     has_xm = jnp.where(gx > 0, 1.0, 0.0).astype(F32)
     has_xp = jnp.where(gx < n_gx - 1, 1.0, 0.0).astype(F32)
@@ -109,16 +157,19 @@
 
     zeros_side = jnp.zeros((4, 8, LANES), F32)
     outside = pl.ds(pl.multiple_of(24 * gy, 8), 8)
-    for buf, count in [(mod_buf, 1)] + [(fields.at[e], 3) for e in range(N_EX - 1)]:
+    padded = [(mod_buf, 1), (basis, N_BASIS)] + [(fields.at[e], 3) for e in range(N_FIELD)]
+    for buf, count in padded:
         for c in range(count):
             buf[c, 1:5, outside, :] = zeros_side
 
-    level = density[...].astype(F32) / 15.0
+    for fetch in fetches:
+        fetch.wait()
+    level = in_density[...].astype(F32) / 15.0
     mod = 0.05 + 0.95 * level * level * level
     mod_buf[0, 1:5, 8:24, :] = mod
-    fixed4 = PENALTY * fixed_mask[...].astype(F32)
-    load_scale = 0.25 + load_mask[...].astype(F32)
-    load = [forces[c] * load_scale for c in range(3)]
+    fixed4 = PENALTY * in_fixed[...].astype(F32)
+    load_scale = 0.25 + in_load[...].astype(F32)
+    load = [in_forces[c] * load_scale for c in range(3)]
 
     def pack_side(values, lane):
         total = None
@@ -142,7 +193,8 @@
         copy.start()
         return copy
 
-    def start_halo(e, buf, values, with_edges):
+    def start_halo(e, buf, values, groups):
+        edge = edge_recv.at[e] if len(values) <= 3 else basis_edge
         copies = [
             remote(e, 0, buf.at[:, 4, 8:24, :], buf.at[:, 0, 8:24, :], (gx_up, gy, gz)),
             remote(e, 1, buf.at[:, 1, 8:24, :], buf.at[:, 5, 8:24, :], (gx_dn, gy, gz)),
@@ -155,7 +207,7 @@
         copies.append(
             remote(e, 3, pack_send.at[e, 1], pack_recv.at[e, 1], (gx, gy, gz_dn))
         )
-        if with_edges:
+        if groups is not None:
             copies.append(
                 remote(e, 4, pack_send.at[e, 0], pack_recv.at[e, 2], (gx_dn, gy, gz_up))
             )
@@ -171,8 +223,13 @@
                 remote(
                     e,
                     7,
-                    buf.at[gy, 1 + 3 * gy, pl.ds(pl.multiple_of(16 - 8 * gy, 8), 8), :],
-                    edge_recv.at[e],
+                    buf.at[
+                        pl.ds(len(groups[0]) * gy, len(groups[0])),
+                        1 + 3 * gy,
+                        pl.ds(pl.multiple_of(16 - 8 * gy, 8), 8),
+                        :,
+                    ],
+                    edge,
                     (gx_side, gy_other, gz),
                 )
             )
@@ -187,46 +244,47 @@
         )
         return copies
 
-    def finish_halo(e, buf, copies, with_edges):
+    def finish_halo(e, buf, low_to, high_to, copies, groups):
         for copy in copies:
             copy.wait()
         count = buf.shape[0]
         for c in range(count):
             buf[c, 0, 8:24, :] = buf[c, 0, 8:24, :] * has_xm
             buf[c, 5, 8:24, :] = buf[c, 5, 8:24, :] * has_xp
+
+        def spread_to(target, c, x, rows, pack, j):
+            target[c, x, rows, :] = jnp.broadcast_to(pack[:, j : j + 1], (8, LANES))
+
         low = pack_recv[e, 0] * has_zm
         high = pack_recv[e, 1] * has_zp
-        target_low = low_z if with_edges else mod_low
-        target_high = high_z
+        tiles = [slice(8, 16), slice(16, 24)]
         for c in range(count):
             for x in range(4):
                 for t in range(2):
-                    j = 8 * c + 2 * x + t
-                    rows = slice(8 + 8 * t, 16 + 8 * t)
-                    target_low[c, 1 + x, rows, :] = jnp.broadcast_to(low[:, j : j + 1], (8, LANES))
-                    target_high[c, 1 + x, rows, :] = jnp.broadcast_to(
-                        high[:, j : j + 1], (8, LANES)
-                    )
-        if with_edges:
+                    spread_to(low_to, c, 1 + x, tiles[t], low, 8 * c + 2 * x + t)
+                    spread_to(high_to, c, 1 + x, tiles[t], high, 8 * c + 2 * x + t)
+        if groups is not None:
+            of_x, of_y, of_z = groups
             low_x = pack_recv[e, 2] * (has_xp * has_zm)
             high_x = pack_recv[e, 3] * (has_xm * has_zp)
             side = pack_recv[e, 4]
             low_y = side * (is_y0 * has_zm)
             high_y = side * (is_y1 * has_zp)
             for t in range(2):
-                rows = slice(8 + 8 * t, 16 + 8 * t)
-                j = t
-                low_z[0, 5, rows, :] = jnp.broadcast_to(low_x[:, j : j + 1], (8, LANES))
-                j = 8 * 2 + 2 * 3 + t
-                high_z[2, 0, rows, :] = jnp.broadcast_to(high_x[:, j : j + 1], (8, LANES))
+                for c in of_x:
+                    spread_to(low_to, c, 5, tiles[t], low_x, 8 * c + t)
+                for c in of_z:
+                    spread_to(high_to, c, 0, tiles[t], high_x, 8 * c + 6 + t)
             for x in range(4):
-                j = 8 + 2 * x
-                low_z[1, 1 + x, 24:32, :] = jnp.broadcast_to(low_y[:, j : j + 1], (8, LANES))
-                j = 8 * 2 + 2 * x + 1
-                high_z[2, 1 + x, 0:8, :] = jnp.broadcast_to(high_y[:, j : j + 1], (8, LANES))
-            corner = edge_recv[e]
-            buf[1, 0, 24:32, :] = corner * (is_y0 * has_xm)
-            buf[0, 5, 0:8, :] = corner * (is_y1 * has_xp)
+                for c in of_y:
+                    spread_to(low_to, c, 1 + x, slice(24, 32), low_y, 8 * c + 2 * x)
+                for c in of_z:
+                    spread_to(high_to, c, 1 + x, slice(0, 8), high_y, 8 * c + 2 * x + 1)
+            edge = edge_recv.at[e] if count <= 3 else basis_edge
+            for k, c in enumerate(of_y):
+                buf[c, 0, 24:32, :] = edge[k] * (is_y0 * has_xm)
+            for k, c in enumerate(of_x):
+                buf[c, 5, 0:8, :] = edge[k] * (is_y1 * has_xp)
 
     def before(value, low):
         return jnp.where(first_lane, low, pltpu.roll(value, 1, 2))
@@ -239,7 +297,7 @@
             fields[e, c, 1:5, 8:24, :] = values[c]
 
     def stiffness(e):
-        buf = fields.at[e]
+        buf, low_z, high_z = (fields.at[e], low_all.at[e], high_all.at[e])
         u_z = buf[2, 0:5, 0:24, :]
         up_z = jnp.where(wide_lane, high_z[2, 0:5, 0:24, :], pltpu.roll(u_z, LANES - 1, 2))
         spread = (
@@ -284,7 +342,10 @@
 
     me_group = gy * n_gz + gz
 
-    def gather_rows(i, row):
+    def far_first(step):
+        return wrap(step + n_gx // 2, n_gx - 1) + 1
+
+    def rows_begin(i, row):
         row_send[i, 0] = row
         group_recv[i, me_group] = row
 
@@ -302,7 +363,9 @@
             group_copy(step).start()
             return carry
 
-        lax.fori_loop(1, n_group, start_group, 0)
+        lax.fori_loop(1, n_group, start_group, 0, unroll=True)
+
+    def rows_middle(i):
         most = group_recv.at[i, pl.ds(0, n_group - 1)]
         pltpu.make_async_copy(most, most, row_recv_sem.at[i, 0]).wait()
         total = group_recv[i, 0]
@@ -317,12 +380,15 @@
                 dst_ref=slab_recv.at[i, gx],
                 send_sem=row_send_sem.at[i, 1],
                 recv_sem=row_recv_sem.at[i, 1],
-                device_id=(wrap(gx + step, n_gx), gy, gz),
+                device_id=(wrap(gx + far_first(step), n_gx), gy, gz),
                 device_id_type=MESH,
             ).start()
             return carry
 
-        lax.fori_loop(1, n_gx, start_slab, 0)
+        lax.fori_loop(0, n_gx - 1, start_slab, 0, unroll=True)
+
+    def rows_end(i):
+        most = group_recv.at[i, pl.ds(0, n_group - 1)]
         rest = slab_recv.at[i, pl.ds(0, n_gx - 1)]
         pltpu.make_async_copy(rest, rest, row_recv_sem.at[i, 1]).wait()
         pltpu.make_async_copy(most, most, row_send_sem.at[i, 0]).wait()
@@ -410,16 +476,18 @@
     def nearby(solved):
         turned = pltpu.roll(solved, wrap(1 - gx, LANES), 1)
         return [
-            [jnp.broadcast_to(turned[c : c + 1, b : b + 1], (16, LANES)) for c in range(3)]
+            [jnp.broadcast_to(turned[c : c + 1, b : b + 1], (32, LANES)) for c in range(3)]
             for b in range(3)
         ]
 
-    pl.semaphore_wait(barrier, n_gx - 1 + n_group - 1 + 3)
-
-    copies = start_halo(0, mod_buf, [mod], False)
-    finish_halo(0, mod_buf, copies, False)
+    pl.semaphore_wait(barrier, len(near))
+
+    plain = ((0,), (1,), (2,))
+    copies = start_halo(0, mod_buf, [mod], None)
+    flood(0, 4)
+    finish_halo(0, mod_buf, mod_low, mod_high, copies, None)
     mod_zm = before(mod, mod_low[0, 1:5, 8:24, :])
-    mod_zp = after(mod, high_z[0, 1:5, 8:24, :])
+    mod_zp = after(mod, mod_high[0, 1:5, 8:24, :])
     mod_xm, mod_xp = (mod_buf[0, 0:4, 8:24, :], mod_buf[0, 2:6, 8:24, :])
     mod_ym, mod_yp = (mod_buf[0, 1:5, 7:23, :], mod_buf[0, 1:5, 9:25, :])
     couplings = [0.5 * (mod + v) for v in (mod_xm, mod_xp, mod_ym, mod_yp, mod_zm, mod_zp)]
@@ -433,7 +501,8 @@
 
     first = [load[c] * dinv_buf[c] for c in range(3)]
     set_field(0, first)
-    copies = start_halo(1, fields.at[0], first, True)
+    copies = start_halo(1, fields.at[0], first, plain)
+    flood(4, len(floods))
 
     low_y_edge = jnp.where(y3 == 0, is_y0, 0.0)
     high_y_edge = jnp.where(y3 == 15, is_y1, 0.0)
@@ -452,7 +521,6 @@
     )
     half = LAME * mod
     half_xm = LAME * mod_xm
-    keep[0] = bound
     rows_buf[...] = jnp.zeros((16, LANES), F32)
     put_sum(0, bound + half_xm * first_x + half * last_x)
     put_sum(1, bound + half * high_y_edge)
@@ -463,48 +531,80 @@
     put_sum(6, couplings[1][3])
     put_sum(7, couplings[1][3] + half[3])
 
-    def image_of(coarse):
-        under, own, over = coarse
-        bound = keep[0]
-        mod = mod_buf[0, 1:5, 8:24, :]
-        half = LAME * mod
-        half_xm = LAME * mod_buf[0, 0:4, 8:24, :]
-        half_ym = LAME * mod_buf[0, 1:5, 7:23, :]
-        half_zm = LAME * before(mod, mod_low[0, 1:5, 8:24, :])
-        low_x, high_x = (coef[0], coef[1])
-        inner_xm = half_xm * (1.0 - first_x)
-        down_y, down_z = (half - half_ym, half - half_zm)
-        image_x = (
-            (bound + half_xm * first_x + half * last_x) * own[0]
-            + (half - inner_xm) * (high_y_edge * own[1] + high_z_edge * own[2])
-            - first_x
-            * (
-                (low_x + half_xm) * under[0]
-                + half_xm * (high_y_edge * under[1] + high_z_edge * under[2])
+    dinv = [dinv_buf[c] for c in range(3)]
+    inner_xm = half_xm * (1.0 - first_x)
+    pieces = [
+        dinv[0] * (bound + half_xm * first_x + half * last_x),
+        dinv[0] * (half - inner_xm),
+        dinv[0] * (first_x * (couplings[0] + half_xm) + last_x * (couplings[1] + half)),
+        dinv[0] * first_x * half_xm,
+        dinv[1] * (bound + half * high_y_edge),
+        dinv[1] * (half - LAME * mod_ym),
+        dinv[1] * (first_x * couplings[0] + last_x * couplings[1]),
+        dinv[2] * (bound + half * high_z_edge),
+        dinv[2] * (half - LAME * mod_zm),
+        dinv[2] * (first_x * couplings[0] + last_x * couplings[1]),
+    ]
+    for c in range(N_BASIS):
+        basis[c, 1:5, 8:24, :] = pieces[c]
+    basis_groups = ((0, 1, 2, 3), (4, 5, 6), (7, 8, 9))
+
+    whole = (6, 32, LANES)
+    x6 = lax.broadcasted_iota(jnp.int32, whole, 0)
+    y6 = lax.broadcasted_iota(jnp.int32, whole, 1)
+    lane6 = lax.broadcasted_iota(jnp.int32, whole, 2)
+
+    def coarse_fields(near):
+        under, here, over = near
+        inside = jnp.where(y6 < 8, is_y1, jnp.where(y6 >= 24, is_y0, 1.0))
+        top_y = jnp.where(y6 == 23, is_y1, 0.0)
+        top_z = jnp.where(lane6 == LANES - 1, 1.0 - has_zp, 0.0)
+        own = [jnp.where(x6 == 0, under[c], jnp.where(x6 == 5, over[c], here[c])) for c in range(3)]
+        other = [
+            jnp.where(
+                x6 == 1,
+                under[c],
+                jnp.where(
+                    x6 == 4, over[c], jnp.where(jnp.logical_or(x6 == 0, x6 == 5), here[c], 0.0)
+                ),
             )
-            - last_x * (high_x + half) * over[0]
-        )
-        image_y = (
-            (bound + half * high_y_edge) * own[1]
-            + down_y * (last_x * (own[0] - over[0]) + high_z_edge * own[2])
-            - first_x * low_x * under[1]
-            - last_x * high_x * over[1]
-        )
-        image_z = (
-            (bound + half * high_z_edge) * own[2]
-            + down_z * (last_x * (own[0] - over[0]) + high_y_edge * own[1])
-            - first_x * low_x * under[2]
-            - last_x * high_x * over[2]
-        )
-        return [image_x, image_y, image_z]
-
-    finish_halo(1, fields.at[0], copies, True)
+            for c in range(3)
+        ]
+        drop = jnp.where(x6 == 4, here[0] - over[0], jnp.where(x6 == 0, under[0] - here[0], 0.0))
+        own_y, other_y = (top_y * own[1], top_y * other[1])
+        own_z, other_z = (top_z * own[2], top_z * other[2])
+
+        def evaluate(b, scale, with_z):
+            t_own = own_y + own_z if with_z else own_y
+            t_other = other_y + other_z if with_z else other_y
+            drop_y = drop + own_z if with_z else drop
+            held = inside if scale is None else inside * scale
+            return [
+                (held - b[0]) * own[0] - b[1] * t_own + b[2] * other[0] + b[3] * t_other,
+                (held - b[4]) * own[1] - b[5] * drop_y + b[6] * other[1],
+                (held - b[7]) * own[2] - b[8] * (drop + own_y) + b[9] * other[2],
+            ]
+
+        return (
+            evaluate(basis, None, True),
+            evaluate(basis_low, has_zm, False),
+            evaluate(basis_high, has_zp, False),
+        )
+
+    finish_halo(1, fields.at[0], low_all.at[0], high_all.at[0], copies, plain)
     image_first = stiffness(0)
     rest = [load[c] - image_first[c] for c in range(3)]
     for c in range(3):
         put_sum(8 + c, rest[c])
-        keep[1 + c] = rest[c]
-    gather_rows(0, make_row())
+    rows_begin(0, make_row())
+    partial = [first[c] + dinv_buf[c] * rest[c] for c in range(3)]
+    set_field(1, partial)
+    copies = start_halo(2, fields.at[1], partial, plain)
+    more = start_halo(3, basis, [basis[c, 1:5, 8:24, :] for c in range(N_BASIS)], basis_groups)
+    rows_middle(0)
+    finish_halo(2, fields.at[1], low_all.at[1], high_all.at[1], copies, plain)
+    finish_halo(3, basis, basis_low, basis_high, more, basis_groups)
+    rows_end(0)
 
     table = slab_rows(0)
     real = lane_row < n_gx
@@ -530,33 +630,34 @@
         stack3(-moved[2], none, -moved[3]),
     ]
     near = nearby(factorise(lower, main, upper, stack3(row[8], row[9], row[10])))
-    coarse_image = image_of(near)
-    precond = []
-    for c in range(3):
-        second = fields[0, c, 1:5, 8:24, :] + near[1][c]
-        precond.append(second + dinv_buf[c] * (keep[1 + c] - coarse_image[c]))
-    set_field(1, precond)
-    copies = start_halo(2, fields.at[1], precond, True)
-    load = [forces[c] * load_scale for c in range(3)]
-    rows_buf[...] = jnp.zeros((16, LANES), F32)
-    put_sum(0, load[0] * precond[0] + load[1] * precond[1] + load[2] * precond[2])
-    finish_halo(2, fields.at[1], copies, True)
+    for target, extra in zip((fields, low_all, high_all), coarse_fields(near)):
+        for c in range(3):
+            target[1, c] = target[1, c] + extra[c]
     image = stiffness(1)
     smooth = []
     for c in range(3):
-        keep[4 + c] = image[c]
+        keep[c] = image[c]
         smooth.append(dinv_buf[c] * image[c])
     set_field(2, smooth)
-    copies = start_halo(3, fields.at[2], smooth, True)
+    copies = start_halo(4, fields.at[2], smooth, plain)
+    rows_buf[...] = jnp.zeros((16, LANES), F32)
     precond = [fields[1, c, 1:5, 8:24, :] for c in range(3)]
+    load = [in_forces[c] * load_scale for c in range(3)]
+    put_sum(0, load[0] * precond[0] + load[1] * precond[1] + load[2] * precond[2])
     put_sum(1, image[0] * precond[0] + image[1] * precond[1] + image[2] * precond[2])
-    finish_halo(3, fields.at[2], copies, True)
+    finish_halo(4, fields.at[2], low_all.at[2], high_all.at[2], copies, plain)
     image_smooth = stiffness(2)
+    change = []
     for c in range(3):
-        remain = keep[4 + c] - image_smooth[c]
-        keep[1 + c] = remain
+        remain = keep[c] - image_smooth[c]
         put_sum(2 + c, remain)
-    gather_rows(1, make_row())
+        change.append(fields[2, c, 1:5, 8:24, :] + dinv_buf[c] * remain)
+    rows_begin(1, make_row())
+    set_field(3, change)
+    copies = start_halo(5, fields.at[3], change, plain)
+    rows_middle(1)
+    finish_halo(5, fields.at[3], low_all.at[3], high_all.at[3], copies, plain)
+    rows_end(1)
 
     table = slab_rows(1)
     row = [jnp.where(real, table[q : q + 1, :], 0.0) for q in range(5)]
@@ -564,31 +665,27 @@
     curve = jnp.sum(row[1], axis=1, keepdims=True)
     step0 = norm_now / curve
     near = nearby(solve_again(stack3(row[2], row[3], row[4])))
-    coarse_image = image_of(near)
+    wide0 = jnp.broadcast_to(step0, (32, LANES))
+    for target, extra in zip((fields, low_all, high_all), coarse_fields(near)):
+        for c in range(3):
+            target[3, c] = target[1, c] - wide0 * (target[3, c] + extra[c])
     wide0 = jnp.broadcast_to(step0, (16, LANES))
-    following = []
+    image_next = stiffness(3)
+    rows_buf[...] = jnp.zeros((16, LANES), F32)
+    norm_part = jnp.zeros(shape, F32)
+    curve_part = jnp.zeros(shape, F32)
     for c in range(3):
-        second = fields[2, c, 1:5, 8:24, :] + near[1][c]
-        change = second + dinv_buf[c] * (keep[1 + c] - coarse_image[c])
-        following.append(fields[1, c, 1:5, 8:24, :] - wide0 * change)
-    set_field(3, following)
-    copies = start_halo(4, fields.at[3], following, True)
-    rows_buf[...] = jnp.zeros((16, LANES), F32)
-    residual = []
-    product = jnp.zeros(shape, F32)
-    for c in range(3):
-        residual.append(forces[c] * load_scale - wide0 * keep[4 + c])
-        product = product + residual[c] * following[c]
-        keep[1 + c] = residual[c]
-    put_sum(0, product)
-    finish_halo(4, fields.at[3], copies, True)
-    image_next = stiffness(3)
-    product = jnp.zeros(shape, F32)
-    for c in range(3):
-        product = product + image_next[c] * fields[3, c, 1:5, 8:24, :]
-        keep[7 + c] = image_next[c]
-    put_sum(1, product)
-    gather_rows(2, make_row())
+        following = fields[3, c, 1:5, 8:24, :]
+        residual = in_forces[c] * load_scale - wide0 * keep[c]
+        norm_part = norm_part + residual * following
+        curve_part = curve_part + image_next[c] * following
+        keep[3 + c] = residual
+        keep[6 + c] = image_next[c]
+    put_sum(0, norm_part)
+    put_sum(1, curve_part)
+    rows_begin(2, make_row())
+    rows_middle(2)
+    rows_end(2)
 
     both = slab_recv[2, 0]
     for k in range(1, n_gx):
@@ -602,7 +699,7 @@
         previous = fields[1, c, 1:5, 8:24, :]
         search = fields[3, c, 1:5, 8:24, :] + wide_ratio * previous
         disp_out[c] = wide0 * previous + wide1 * search
-        res_out[c] = keep[1 + c] - wide1 * (keep[7 + c] + wide_ratio * keep[4 + c])
+        res_out[c] = keep[3 + c] - wide1 * (keep[6 + c] + wide_ratio * keep[c])
 
 
 def solution(mesh):
@@ -619,30 +716,41 @@
         return pl.pallas_call(
             run,
             out_shape=(block, block),
-            in_specs=[vmem] * 4,
+            in_specs=[pl.BlockSpec(memory_space=pl.ANY)] * 4,
             out_specs=(vmem, vmem),
             scratch_shapes=[
                 pltpu.VMEM((1, 6, 32, LANES), F32),
-                pltpu.VMEM((N_EX - 1, 3, 6, 32, LANES), F32),
-                pltpu.VMEM((3, 6, 32, LANES), F32),
-                pltpu.VMEM((3, 6, 32, LANES), F32),
+                pltpu.VMEM((N_FIELD, 3, 6, 32, LANES), F32),
+                pltpu.VMEM((N_FIELD, 3, 6, 32, LANES), F32),
+                pltpu.VMEM((N_FIELD, 3, 6, 32, LANES), F32),
                 pltpu.VMEM((1, 6, 32, LANES), F32),
+                pltpu.VMEM((1, 6, 32, LANES), F32),
+                pltpu.VMEM((N_BASIS, 6, 32, LANES), F32),
+                pltpu.VMEM((N_BASIS, 6, 32, LANES), F32),
+                pltpu.VMEM((N_BASIS, 6, 32, LANES), F32),
                 pltpu.VMEM((N_EX, 2, 8, LANES), F32),
                 pltpu.VMEM((N_EX, 5, 8, LANES), F32),
-                pltpu.VMEM((N_EX, 8, LANES), F32),
+                pltpu.VMEM((N_EX, 1, 8, LANES), F32),
+                pltpu.VMEM((4, 8, LANES), F32),
                 pltpu.VMEM((5, 24, LANES), F32),
                 pltpu.VMEM((7, 4, 16, LANES), F32),
                 pltpu.VMEM((3, 4, 16, LANES), F32),
-                pltpu.VMEM((10, 4, 16, LANES), F32),
+                pltpu.VMEM((9, 4, 16, LANES), F32),
                 pltpu.VMEM((16, LANES), F32),
                 pltpu.VMEM((steps_for(n_gx) + 1, 6, 8, LANES), F32),
                 pltpu.VMEM((3, 2, 1, LANES), F32),
                 pltpu.VMEM((3, n_group, 1, LANES), F32),
                 pltpu.VMEM((3, n_gx, 1, LANES), F32),
+                pltpu.VMEM((4, 16, LANES), jnp.int32),
+                pltpu.VMEM((4, 16, LANES), jnp.int32),
+                pltpu.VMEM((4, 16, LANES), jnp.int32),
+                pltpu.VMEM((3, 4, 16, LANES), F32),
+                pltpu.SemaphoreType.DMA((4,)),
                 pltpu.SemaphoreType.DMA((N_EX, N_MSG)),
                 pltpu.SemaphoreType.DMA((N_EX, N_MSG)),
                 pltpu.SemaphoreType.DMA((3, 2)),
                 pltpu.SemaphoreType.DMA((3, 2)),
+                pltpu.SemaphoreType.REGULAR((8, 2)),
             ],
             compiler_params=pltpu.CompilerParams(collective_id=0, has_side_effects=True),
         )(density, fixed_mask, load_mask, forces)

time: 87.7 us -> 77.8 us (0.89)
  Pallas kernels: 84.6 us -> 74.7 us
    pallas_call x1, Pallas kernels: 84.6 us -> 74.7 us  [body(): pl.pallas_call(run, out_shape=(block, block), in_specs=[pl.BlockSpec(memo...]
where the time goes in v2:
time: 77.8 us; the launch traced here: 77.6 us
  Pallas kernels  74.7 us (96%)
  local copies, waits for them, and re-layouts  2.22 us (3%)
    pallas_call x1, Pallas kernels, body(): pl.pallas_call(run, out_shape=(block, block), in_specs=[pl.BlockSpec(memo...  74.7 us
    unnamed x4, local copies, waits for them, and re-layouts  2.22 us

profile of v2, /device:TPU:1, one launch (start us, length us, event | category | flops | bytes accessed | tf_op | source)
XLA Modules:
  0.0 77.6 jit_solution(5766761744622360545)
XLA Ops:
  0.6 74.7 %shard_map.59 = (f32[3,4,16,128]{3,2,1,0:T(8,128)}, f32[3,4,16,128]{3,2,1,0:T(8,128)}) custom-call(s32[4,16,128]{2,1,0:T(8,128)} %refs_0_.1, s32[4,16,128]{2,1,0:T(8,128)} %refs_1_.1, s32[4,16,128]{2,1,0:T(8,128)} %refs_2_.1, f32[3,4,16,128]{3,2,1,0:T(8,128)} %refs_3_.1), custom_call_target="tpu_custom_call" | custom-call | tf_op jit(solution)/shard_map/pallas_call | solution.py:716
  75.3 0.0 copy-start
  75.3 1.6 %copy.8 = f32[3,4,16,128]{3,2,1,0:T(8,128)} copy(f32[3,4,16,128]{3,2,1,0:T(8,128)} %get-tuple-element.4) | data formatting | bytes 196608
  76.9 0.0 copy-done
  76.9 0.6 copy.9
Async XLA Ops:
  75.3 1.6 %copy-start = (f32[3,4,16,128]{3,2,1,0:T(8,128)S(1)}, f32[3,4,16,128]{3,2,1,0:T(8,128)}, u32[]{:S(2)}) copy-start(f32[3,4,16,128]{3,2,1,0:T(8,128)} %get-tuple-element.5) | copy-start | bytes 294916

commit v3 on v2

--- a/solution.py
+++ b/solution.py
@@ -13,7 +13,9 @@
 LANES = 128
 N_MSG = 9
 N_EX = 6
-N_FIELD = 4
+N_FIELD = 5
+N_ROWS = 104
+FIRST_G = 16
 N_BASIS = 10
 
 
@@ -50,6 +52,7 @@
     dinv_buf,
     keep,
     rows_buf,
+    units,
     pcr_buf,
     row_send,
     group_recv,
@@ -152,12 +155,14 @@
     slot3 = 2 * x3 + jnp.where(y3 >= 8, 1, 0)
     first_lane, last_lane = (lane3 == 0, lane3 == LANES - 1)
     wide_lane = lax.broadcasted_iota(jnp.int32, (5, 24, LANES), 2) == LANES - 1
-    lane2 = lax.broadcasted_iota(jnp.int32, (16, LANES), 1)
-    diag2 = lane2 == lax.broadcasted_iota(jnp.int32, (16, LANES), 0)
+    table_shape = (N_ROWS, LANES)
+    diag2 = lax.broadcasted_iota(jnp.int32, table_shape, 1) == lax.broadcasted_iota(
+        jnp.int32, table_shape, 0
+    )
 
     zeros_side = jnp.zeros((4, 8, LANES), F32)
     outside = pl.ds(pl.multiple_of(24 * gy, 8), 8)
-    padded = [(mod_buf, 1), (basis, N_BASIS)] + [(fields.at[e], 3) for e in range(N_FIELD)]
+    padded = [(mod_buf, 1), (basis, N_BASIS)] + [(fields.at[e], 3) for e in range(4)]
     for buf, count in padded:
         for c in range(count):
             buf[c, 1:5, outside, :] = zeros_side
@@ -334,7 +339,7 @@
         if value.ndim == 3:
             value = value[0] + value[1] + value[2] + value[3]
         value = value[0:8] + value[8:16]
-        rows_buf[q : q + 1, :] = jnp.sum(value, axis=0, keepdims=True)
+        rows_buf[pl.ds(q, 1), :] = jnp.sum(value, axis=0, keepdims=True)
 
     def make_row():
         sums = jnp.sum(rows_buf[...], axis=1, keepdims=True)
@@ -521,7 +526,7 @@
     )
     half = LAME * mod
     half_xm = LAME * mod_xm
-    rows_buf[...] = jnp.zeros((16, LANES), F32)
+    rows_buf[...] = jnp.zeros(table_shape, F32)
     put_sum(0, bound + half_xm * first_x + half * last_x)
     put_sum(1, bound + half * high_y_edge)
     put_sum(2, bound + half * high_z_edge)
@@ -591,6 +596,31 @@
             evaluate(basis_high, has_zp, False),
         )
 
+    def dot3(left, right):
+        return left[0] * right[0] + left[1] * right[1] + left[2] * right[2]
+
+    def unit_products(first_unit, last_unit):
+        def body(i, carry):
+            near = [
+                [
+                    jnp.broadcast_to(jnp.where(i == 3 * b + c, 1.0, 0.0).astype(F32), (32, LANES))
+                    for c in range(3)
+                ]
+                for b in range(3)
+            ]
+            for target, value in zip((fields, low_all, high_all), coarse_fields(near)):
+                for c in range(3):
+                    target[4, c] = value[c]
+            for c in range(3):
+                units[i, c] = fields[4, c, 1:5, 8:24, :]
+            image = stiffness(4)
+            for j in range(9):
+                put_sum(FIRST_G + 9 * i + j, dot3(image, [units[j, c] for c in range(3)]))
+            return carry
+
+        lax.fori_loop(first_unit, last_unit, body, 0)
+
+    units[...] = jnp.zeros((9, 3, 4, 16, LANES), F32)
     finish_halo(1, fields.at[0], low_all.at[0], high_all.at[0], copies, plain)
     image_first = stiffness(0)
     rest = [load[c] - image_first[c] for c in range(3)]
@@ -604,6 +634,7 @@
     rows_middle(0)
     finish_halo(2, fields.at[1], low_all.at[1], high_all.at[1], copies, plain)
     finish_halo(3, basis, basis_low, basis_high, more, basis_groups)
+    unit_products(0, 3)
     rows_end(0)
 
     table = slab_rows(0)
@@ -640,11 +671,11 @@
         smooth.append(dinv_buf[c] * image[c])
     set_field(2, smooth)
     copies = start_halo(4, fields.at[2], smooth, plain)
-    rows_buf[...] = jnp.zeros((16, LANES), F32)
     precond = [fields[1, c, 1:5, 8:24, :] for c in range(3)]
     load = [in_forces[c] * load_scale for c in range(3)]
     put_sum(0, load[0] * precond[0] + load[1] * precond[1] + load[2] * precond[2])
     put_sum(1, image[0] * precond[0] + image[1] * precond[1] + image[2] * precond[2])
+    unit_products(3, 6)
     finish_halo(4, fields.at[2], low_all.at[2], high_all.at[2], copies, plain)
     image_smooth = stiffness(2)
     change = []
@@ -652,54 +683,58 @@
         remain = keep[c] - image_smooth[c]
         put_sum(2 + c, remain)
         change.append(fields[2, c, 1:5, 8:24, :] + dinv_buf[c] * remain)
-    rows_begin(1, make_row())
     set_field(3, change)
     copies = start_halo(5, fields.at[3], change, plain)
+    put_sum(5, dot3([keep[c] for c in range(3)], change))
+    unit_products(6, 9)
+    finish_halo(5, fields.at[3], low_all.at[3], high_all.at[3], copies, plain)
+    image_change = stiffness(3)
+    put_sum(6, dot3(image_change, [fields[3, c, 1:5, 8:24, :] for c in range(3)]))
+    for j in range(9):
+        put_sum(7 + j, dot3(image_change, [units[j, c] for c in range(3)]))
+    rows_begin(1, make_row())
     rows_middle(1)
-    finish_halo(5, fields.at[3], low_all.at[3], high_all.at[3], copies, plain)
     rows_end(1)
 
     table = slab_rows(1)
-    row = [jnp.where(real, table[q : q + 1, :], 0.0) for q in range(5)]
-    norm_now = jnp.sum(row[0], axis=1, keepdims=True)
-    curve = jnp.sum(row[1], axis=1, keepdims=True)
+    row = [table[q : q + 1, :] for q in range(FIRST_G)]
+    solved = solve_again(stack3(row[2], row[3], row[4]))
+    around = [pltpu.roll(solved, 1, 1), solved, pltpu.roll(solved, LANES - 1, 1)]
+    at = [around[b][c : c + 1, :] for b in range(3) for c in range(3)]
+    mixed = row[6]
+    for i in range(9):
+        inner = 2.0 * row[7 + i]
+        for j in range(i + 1):
+            q = FIRST_G + 9 * i + j
+            inner = inner + (2.0 if j < i else 1.0) * table[q : q + 1, :] * at[j]
+        mixed = mixed + at[i] * inner
+    cross = row[5] + row[2] * at[3] + row[3] * at[4] + row[4] * at[5]
+
+    def over_slabs(value):
+        return jnp.sum(value, axis=1, keepdims=True)
+
+    norm_now, curve = (over_slabs(row[0]), over_slabs(row[1]))
+    cross, mixed = (over_slabs(cross), over_slabs(mixed))
     step0 = norm_now / curve
-    near = nearby(solve_again(stack3(row[2], row[3], row[4])))
+    norm_next = step0 * step0 * cross - norm_now
+    curve_next = curve - 2.0 * step0 * cross + step0 * step0 * mixed
+    ratio = norm_next / norm_now
+    step1 = norm_next / (curve_next - ratio * norm_next / step0)
+    near = nearby(solved)
     wide0 = jnp.broadcast_to(step0, (32, LANES))
     for target, extra in zip((fields, low_all, high_all), coarse_fields(near)):
         for c in range(3):
             target[3, c] = target[1, c] - wide0 * (target[3, c] + extra[c])
+    image_next = stiffness(3)
     wide0 = jnp.broadcast_to(step0, (16, LANES))
-    image_next = stiffness(3)
-    rows_buf[...] = jnp.zeros((16, LANES), F32)
-    norm_part = jnp.zeros(shape, F32)
-    curve_part = jnp.zeros(shape, F32)
-    for c in range(3):
-        following = fields[3, c, 1:5, 8:24, :]
-        residual = in_forces[c] * load_scale - wide0 * keep[c]
-        norm_part = norm_part + residual * following
-        curve_part = curve_part + image_next[c] * following
-        keep[3 + c] = residual
-        keep[6 + c] = image_next[c]
-    put_sum(0, norm_part)
-    put_sum(1, curve_part)
-    rows_begin(2, make_row())
-    rows_middle(2)
-    rows_end(2)
-
-    both = slab_recv[2, 0]
-    for k in range(1, n_gx):
-        both = both + slab_recv[2, k]
-    norm_next, curve_next = (both[0:1, 0:1], both[0:1, 1:2])
-    ratio = norm_next / norm_now
-    step1 = norm_next / (curve_next - ratio * norm_next / step0)
     wide_ratio = jnp.broadcast_to(ratio, (16, LANES))
     wide1 = jnp.broadcast_to(step1, (16, LANES))
     for c in range(3):
         previous = fields[1, c, 1:5, 8:24, :]
         search = fields[3, c, 1:5, 8:24, :] + wide_ratio * previous
         disp_out[c] = wide0 * previous + wide1 * search
-        res_out[c] = keep[3 + c] - wide1 * (keep[6 + c] + wide_ratio * keep[c])
+        residual = in_forces[c] * load_scale - wide0 * keep[c]
+        res_out[c] = residual - wide1 * (image_next[c] + wide_ratio * keep[c])
 
 
 def solution(mesh):
@@ -735,12 +770,13 @@
                 pltpu.VMEM((5, 24, LANES), F32),
                 pltpu.VMEM((7, 4, 16, LANES), F32),
                 pltpu.VMEM((3, 4, 16, LANES), F32),
-                pltpu.VMEM((9, 4, 16, LANES), F32),
-                pltpu.VMEM((16, LANES), F32),
+                pltpu.VMEM((3, 4, 16, LANES), F32),
+                pltpu.VMEM((N_ROWS, LANES), F32),
+                pltpu.VMEM((9, 3, 4, 16, LANES), F32),
                 pltpu.VMEM((steps_for(n_gx) + 1, 6, 8, LANES), F32),
-                pltpu.VMEM((3, 2, 1, LANES), F32),
-                pltpu.VMEM((3, n_group, 1, LANES), F32),
-                pltpu.VMEM((3, n_gx, 1, LANES), F32),
+                pltpu.VMEM((2, 2, 1, LANES), F32),
+                pltpu.VMEM((2, n_group, 1, LANES), F32),
+                pltpu.VMEM((2, n_gx, 1, LANES), F32),
                 pltpu.VMEM((4, 16, LANES), jnp.int32),
                 pltpu.VMEM((4, 16, LANES), jnp.int32),
                 pltpu.VMEM((4, 16, LANES), jnp.int32),
@@ -748,8 +784,8 @@
                 pltpu.SemaphoreType.DMA((4,)),
                 pltpu.SemaphoreType.DMA((N_EX, N_MSG)),
                 pltpu.SemaphoreType.DMA((N_EX, N_MSG)),
-                pltpu.SemaphoreType.DMA((3, 2)),
-                pltpu.SemaphoreType.DMA((3, 2)),
+                pltpu.SemaphoreType.DMA((2, 2)),
+                pltpu.SemaphoreType.DMA((2, 2)),
                 pltpu.SemaphoreType.REGULAR((8, 2)),
             ],
             compiler_params=pltpu.CompilerParams(collective_id=0, has_side_effects=True),

time: 77.8 us -> 70.7 us (0.909)
  Pallas kernels: 74.7 us -> 67.6 us
    pallas_call x1, Pallas kernels: 74.7 us -> 67.6 us  [body(): pl.pallas_call(run, out_shape=(block, block), in_specs=[pl.BlockSpec(memo...]
where the time goes in v3:
time: 70.7 us; the launch traced here: 70.5 us
  Pallas kernels  67.6 us (96%)
  local copies, waits for them, and re-layouts  2.22 us (3%)
    pallas_call x1, Pallas kernels, body(): pl.pallas_call(run, out_shape=(block, block), in_specs=[pl.BlockSpec(memo...  67.6 us
    unnamed x4, local copies, waits for them, and re-layouts  2.22 us

profile of v3, /device:TPU:1, one launch (start us, length us, event | category | flops | bytes accessed | tf_op | source)
XLA Modules:
  0.0 70.5 jit_solution(16459819625598350454)
XLA Ops:
  0.6 67.6 %shard_map.59 = (f32[3,4,16,128]{3,2,1,0:T(8,128)}, f32[3,4,16,128]{3,2,1,0:T(8,128)}) custom-call(s32[4,16,128]{2,1,0:T(8,128)} %refs_0_.1, s32[4,16,128]{2,1,0:T(8,128)} %refs_1_.1, s32[4,16,128]{2,1,0:T(8,128)} %refs_2_.1, f32[3,4,16,128]{3,2,1,0:T(8,128)} %refs_3_.1), custom_call_target="tpu_custom_call" | custom-call | tf_op jit(solution)/shard_map/pallas_call | solution.py:751
  68.3 0.0 copy-start
  68.3 1.6 %copy.8 = f32[3,4,16,128]{3,2,1,0:T(8,128)} copy(f32[3,4,16,128]{3,2,1,0:T(8,128)} %get-tuple-element.4) | data formatting | bytes 196608
  69.8 0.0 copy-done
  69.8 0.6 copy.9
Async XLA Ops:
  68.3 1.6 %copy-start = (f32[3,4,16,128]{3,2,1,0:T(8,128)S(1)}, f32[3,4,16,128]{3,2,1,0:T(8,128)}, u32[]{:S(2)}) copy-start(f32[3,4,16,128]{3,2,1,0:T(8,128)} %get-tuple-element.5) | copy-start | bytes 294916

commit v4 on v3

--- a/solution.py
+++ b/solution.py
@@ -741,7 +741,7 @@
     sizes = tuple(mesh.shape[name] for name in ("gx", "gy", "gz"))
     n_gx, n_gy, n_gz = sizes
     n_group = n_gy * n_gz
-    block = jax.ShapeDtypeStruct((3, 4, 16, LANES), F32)
+    place = pltpu.VMEM((3, 4, 16, LANES), F32)
     vmem = pl.BlockSpec(memory_space=pltpu.VMEM)
 
     def body(density, fixed_mask, load_mask, forces):
@@ -750,7 +750,7 @@
 
         return pl.pallas_call(
             run,
-            out_shape=(block, block),
+            out_shape=(place, place),
             in_specs=[pl.BlockSpec(memory_space=pl.ANY)] * 4,
             out_specs=(vmem, vmem),
             scratch_shapes=[

time: 70.7 us -> 69.1 us (0.977)
  local copies, waits for them, and re-layouts: 2.22 us -> 1.28 us
    unnamed x4 -> x2, local copies, waits for them, and re-layouts: 2.22 us -> 1.28 us
where the time goes in v4:
time: 69.1 us; the launch traced here: 68.9 us
  Pallas kernels  67 us (97%)
  local copies, waits for them, and re-layouts  1.28 us (2%)
    pallas_call x1, Pallas kernels, body(): pl.pallas_call(run, out_shape=(place, place), in_specs=[pl.BlockSpec(memo...  67 us

profile of v4, /device:TPU:1, one launch (start us, length us, event | category | flops | bytes accessed | tf_op | source)
XLA Modules:
  0.0 68.9 jit_solution(1450746960692657449)
XLA Ops:
  0.6 67.0 %shard_map.59 = (f32[3,4,16,128]{3,2,1,0:T(8,128)S(1)}, f32[3,4,16,128]{3,2,1,0:T(8,128)S(1)}) custom-call(s32[4,16,128]{2,1,0:T(8,128)} %refs_0_.1, s32[4,16,128]{2,1,0:T(8,128)} %refs_1_.1, s32[4,16,128]{2,1,0:T(8,128)} %refs_2_.1, f32[3,4,16,128]{3,2,1,0:T(8,128)} %refs_3_.1), custom_call_target="tpu_custom_call" | custom-call | tf_op jit(solution)/shard_map/pallas_call | solution.py:751
  67.6 0.6 copy.8
  68.3 0.6 copy.9
